TPU v7x, 256 devices: a whole 4x4x8 slice. The times are simulated.
256 devices in a mesh: seq: 64 (over z, x, y_hi), head: 4 (over y_lo, core).
Axes of the slice: x: 4, y: 4 (y_hi: 2, y_lo: 2; y = y_hi * 2 + y_lo), z: 8, core: 2. Of those that a mesh axis runs over, the one named last changes fastest.
Arguments:
- queries: bfloat16 [16384, 4096], P('seq', 'head'), may hold values from -48 to 48
- key_rows: bfloat16 [16384, 4096], P('seq', 'head'), may hold values from -4 to 4
- value_rows: bfloat16 [16384, 4096], P('seq', 'head'), may hold values from -6 to 6
- out_grad: bfloat16 [16384, 2048], P('seq', 'head'), may hold values from -6 to 6
- out_proj: bfloat16 [4096, 2048], P('head'), may hold values from -0.125 to 0.125
- section_table: int32 [32, 3], P('head'), may hold values 0 or 1
- block_active: int32 [64, 3], P('seq'), may hold values 0 or 1
Outputs:
- query_grad: bfloat16 [16384, 4096], P('seq', 'head')
- key_grad: bfloat16 [16384, 4096], P('seq', 'head')
- value_grad: bfloat16 [16384, 4096], P('seq', 'head')
All inputs are finite; a program needn't handle non-finite values.
Results may differ from a plain program's by a relative error of at most 0.008.
Values may be sent and summed in bfloat16 or wider, within the bound.
A program may use at most 64 MiB of HBM per device.

v0:
```python
from functools import reduce
import math

import jax
import jax.numpy as jnp
from jax import lax
from jax.sharding import PartitionSpec as P

BLK = 256
HDIM = 128
SECTIONS = 3


def in_order(pieces, dim):
    pieces = jnp.moveaxis(pieces, 0, dim)
    lengths = pieces.shape
    return pieces.reshape(*lengths[:dim], lengths[dim] * lengths[dim + 1], *lengths[dim + 2 :])


def sent_to_all(shard, axis):
    copies = jnp.broadcast_to(shard, (lax.axis_size(axis), *shard.shape))
    return lax.all_to_all(copies, axis, split_axis=0, concat_axis=0, tiled=True)


def collect(shard, axis, dim):
    return in_order(sent_to_all(shard, axis), dim)


def shifted(value, axis, steps):
    count = lax.axis_size(axis)
    initial, last = (max(0, -steps), min(count, count - steps))
    return lax.ppermute(value, axis, [(source, source + steps) for source in range(initial, last)])


def split_heads(matrix):
    row_count, col_count = matrix.shape
    return matrix.reshape(row_count // BLK, BLK, col_count // HDIM, HDIM)


def join_heads(blocks):
    block_count, block_rows, head_count, head_size = blocks.shape
    return blocks.reshape(block_count * block_rows, head_count * head_size)


def body(queries, key_rows, value_rows, out_grad, out_proj, section_table, block_active):
    score_scale = 1.0 / math.sqrt(HDIM)
    seq_count = lax.axis_size("seq")
    position = lax.axis_index("seq")
    span_list = [seq_count // 2 ** (section_index + 1) for section_index in range(SECTIONS)]
    hop_list = [
        span_list[section_index]
        - (span_list[section_index + 1] if section_index + 1 < SECTIONS else 0)
        for section_index in range(SECTIONS)
    ]
    attn_grad = lax.dot_general(
        collect(out_grad, "head", 1),
        out_proj,
        (((1,), (1,)), ((), ())),
        preferred_element_type=jnp.float32,
    ).astype(jnp.bfloat16)
    remote = [None] * SECTIONS
    carry_keys = key_rows
    carry_values = value_rows
    for section_index in reversed(range(SECTIONS)):
        carry_keys, carry_values = shifted(
            (carry_keys, carry_values), "seq", hop_list[section_index]
        )
        remote[section_index] = (carry_keys, carry_values)
    query_blocks = split_heads(queries)
    grad_blocks = split_heads(attn_grad)
    row_index = lax.broadcasted_iota(jnp.int32, (BLK, BLK), 0)
    col_index = lax.broadcasted_iota(jnp.int32, (BLK, BLK), 1)
    causal = (row_index >= col_index)[None, None]
    key_sets = [(split_heads(key_rows), split_heads(value_rows), causal)]
    for section_index in range(SECTIONS):
        usable = (
            section_table[:, section_index][None, :] * block_active[:, section_index][:, None] > 0
        ) & (position >= span_list[section_index])
        key_sets.append(
            (
                split_heads(remote[section_index][0]),
                split_heads(remote[section_index][1]),
                usable[:, :, None, None],
            )
        )
    logits = []
    for key_entry in key_sets:
        raw_scores = (
            jnp.einsum(
                "bihd,bjhd->bhij", query_blocks, key_entry[0], preferred_element_type=jnp.float32
            )
            * score_scale
        )
        logits.append(jnp.where(key_entry[2], raw_scores, -1e30))
    row_max = reduce(jnp.maximum, [jnp.max(logit_set, axis=-1) for logit_set in logits])
    row_sum = reduce(
        jnp.add, [jnp.sum(jnp.exp(logit_set - row_max[..., None]), axis=-1) for logit_set in logits]
    )
    log_norm = row_max + jnp.log(row_sum)
    probs_list = [
        jnp.where(key_entry[2], jnp.exp(logit_set - log_norm[..., None]), 0.0)
        for logit_set, key_entry in zip(logits, key_sets)
    ]
    weight_list = [prob_set.astype(jnp.bfloat16) for prob_set in probs_list]
    context = reduce(
        jnp.add,
        [
            jnp.einsum(
                "bhij,bjhd->bihd", weight_set, key_entry[1], preferred_element_type=jnp.float32
            )
            for weight_set, key_entry in zip(weight_list, key_sets)
        ],
    )
    row_delta = jnp.swapaxes(jnp.sum(grad_blocks.astype(jnp.float32) * context, axis=-1), 1, 2)
    query_sum = jnp.zeros(query_blocks.shape, jnp.float32)
    partials = []
    for set_index in range(SECTIONS + 1):
        key_part, value_part, allowed = key_sets[set_index]
        prob_grad = jnp.einsum(
            "bihd,bjhd->bhij", grad_blocks, value_part, preferred_element_type=jnp.float32
        )
        dlogit = (probs_list[set_index] * (prob_grad - row_delta[..., None]) * score_scale).astype(
            jnp.bfloat16
        )
        query_sum = query_sum + jnp.einsum(
            "bhij,bjhd->bihd", dlogit, key_part, preferred_element_type=jnp.float32
        )
        key_term = join_heads(
            jnp.einsum("bhij,bihd->bjhd", dlogit, query_blocks, preferred_element_type=jnp.float32)
        )
        value_term = join_heads(
            jnp.einsum(
                "bhij,bihd->bjhd",
                weight_list[set_index],
                grad_blocks,
                preferred_element_type=jnp.float32,
            )
        )
        if set_index > 0:
            key_term = key_term.astype(jnp.bfloat16)
            value_term = value_term.astype(jnp.bfloat16)
        partials.append((key_term, value_term))
    key_sum, value_sum = partials[0]
    for section_index in range(SECTIONS):
        key_back, value_back = shifted(
            (partials[section_index + 1][0], partials[section_index + 1][1]),
            "seq",
            -span_list[section_index],
        )
        key_sum = key_sum + key_back.astype(jnp.float32)
        value_sum = value_sum + value_back.astype(jnp.float32)
    return (
        join_heads(query_sum).astype(jnp.bfloat16),
        key_sum.astype(jnp.bfloat16),
        value_sum.astype(jnp.bfloat16),
    )


def solution(mesh):
    return jax.shard_map(
        body,
        mesh=mesh,
        in_specs=(
            P("seq", "head"),
            P("seq", "head"),
            P("seq", "head"),
            P("seq", "head"),
            P("head", None),
            P("head", None),
            P("seq", None),
        ),
        out_specs=(P("seq", "head"), P("seq", "head"), P("seq", "head")),
        check_vma=False,
    )
```

profile of v0, /device:TPU:60, one launch (start us, length us, event | category | flops | bytes accessed | tf_op | source)
XLA Modules:
  0.0 246.2 jit_solution(15336996490229027346)
XLA Ops:
  1.9 3.8 %collective-permute-start = (bf16[256,1024]{0,1:T(8,128)(2,1)S(1)}, bf16[256,1024]{0,1:T(8,128)(2,1)}, u32[]{:S(2)}, u32[]{:S(2)}) collective-permute-start(bf16[256,1024]{0,1:T(8,128)(2,1)S(1)} %copy.157), channel_id=1, source_target_pairs={{0,32},{4,36},{8,40},{12,44},{16,48},{20,52},{24,56},{28,60},{32,6... | collective-permute-start | bytes 1572872 | tf_op jit(solution)/shard_map/ppermute | solution.py:32
  7.9 5.1 %all-to-all-start = ((bf16[4,256,512]{1,2,0:T(8,128)(2,1)}), bf16[4,256,512]{1,2,0:T(8,128)(2,1)}, u32[]{:S(2)}, u32[]{:S(2)}) async-start(bf16[4,256,512]{1,2,0:T(8,128)(2,1)} %broadcast_in_dim.79), calls=%async_computation | async-start | bytes 2097152 | tf_op jit(solution)/shard_map/all_to_all | solution.py:22
  13.0 3.8 %collective-permute-start.3 = (bf16[256,1024]{1,0:T(8,128)(2,1)}, bf16[256,1024]{1,0:T(8,128)(2,1)}, u32[]{:S(2)}, u32[]{:S(2)}) collective-permute-start(bf16[256,1024]{1,0:T(8,128)(2,1)} %param.9), channel_id=1, source_target_pairs={{0,32},{4,36},{8,40},{12,44},{16,48},{20,52},{24,56},{28,60},{32,6... | collective-permute-start | bytes 1572872 | tf_op jit(solution)/shard_map/ppermute | solution.py:32
  16.8 2.0 copy.160
  20.2 5.0 %collective-permute-start.1 = (bf16[256,1024]{0,1:T(8,128)(2,1)}, bf16[256,1024]{0,1:T(8,128)(2,1)}, u32[]{:S(2)}, u32[]{:S(2)}) collective-permute-start(bf16[256,1024]{0,1:T(8,128)(2,1)} %collective-permute-done), channel_id=1, source_target_pairs={{0,32},{4,36},{8,40},{12,44},{16,48},{20,52},{24,56},{28,60},{32,6... | collective-permute-start | bytes 1572872 | tf_op jit(solution)/shard_map/ppermute | solution.py:32
  25.3 1.9 and_bitcast_fusion.2
  27.2 2.8 %collective-permute-done.3 = bf16[256,1024]{1,0:T(8,128)(2,1)} collective-permute-done((bf16[256,1024]{1,0:T(8,128)(2,1)}, bf16[256,1024]{1,0:T(8,128)(2,1)}, u32[]{:S(2)}, u32[]{:S(2)}) %collective-permute-start.3) | collective-permute-done | bytes 524320 | tf_op jit(solution)/shard_map/ppermute | solution.py:32
  30.0 4.5 %collective-permute-start.4 = (bf16[256,1024]{1,0:T(8,128)(2,1)}, bf16[256,1024]{1,0:T(8,128)(2,1)}, u32[]{:S(2)}, u32[]{:S(2)}) collective-permute-start(bf16[256,1024]{1,0:T(8,128)(2,1)} %collective-permute-done.3), channel_id=1, source_target_pairs={{0,32},{4,36},{8,40},{12,44},{16,48},{20,52},{24,56},{28,60},{32,6... | collective-permute-start | bytes 1572872 | tf_op jit(solution)/shard_map/ppermute | solution.py:32
  34.4 2.9 %fusion.24 = (f32[8,256]{1,0:T(8,128)S(1)}, f32[8,256,256]{1,2,0:T(8,128)}) fusion(bf16[256,8,128]{0,2,1:T(8,128)(2,1)S(1)} %bitcast.136, bf16[256,8,128]{0,2,1:T(8,128)(2,1)} %bitcast.8, pred[8]{0:T(512)(128)(4,1)S(1)} %get-tuple-element.14), kind=kOutput, calls=%fused_computation.51 | convolution fusion | flops 135788544 | bytes 3153928 | tf_op jit(solution)/shard_map/bihd,bjhd->bhij/dot_general | solution.py:89
  37.4 2.0 copy.87
  39.4 1.8 collective-permute-done.1
  41.2 7.2 %collective-permute-start.2 = (bf16[256,1024]{0,1:T(8,128)(2,1)}, bf16[256,1024]{0,1:T(8,128)(2,1)}, u32[]{:S(2)}, u32[]{:S(2)}) collective-permute-start(bf16[256,1024]{0,1:T(8,128)(2,1)} %collective-permute-done.1), channel_id=1, source_target_pairs={{0,64},{4,68},{8,72},{12,76},{16,80},{20,84},{24,88},{28,92},{32,9... | collective-permute-start | bytes 1572872 | tf_op jit(solution)/shard_map/ppermute | solution.py:32
  48.4 4.6 %convolution_convert_fusion.6 = bf16[256,1024]{1,0:T(8,128)(2,1)} fusion(bf16[256,2048]{0,1:T(8,128)(2,1)} %bitcast.10, bf16[1024,2048]{1,0:T(8,128)(2,1)} %param.11), kind=kOutput, calls=%fused_computation.35 | convolution fusion | flops 1074003968 | bytes 5767168 | tf_op jit(solution)/shard_map/dot_general | solution.py:55
  54.2 2.2 copy.156
  56.5 12.2 %collective-permute-done.4 = bf16[256,1024]{1,0:T(8,128)(2,1)} collective-permute-done((bf16[256,1024]{1,0:T(8,128)(2,1)}, bf16[256,1024]{1,0:T(8,128)(2,1)}, u32[]{:S(2)}, u32[]{:S(2)}) %collective-permute-start.4) | collective-permute-done | bytes 524320 | tf_op jit(solution)/shard_map/ppermute | solution.py:32
  68.7 4.3 %collective-permute-start.5 = (bf16[256,1024]{1,0:T(8,128)(2,1)}, bf16[256,1024]{1,0:T(8,128)(2,1)}, u32[]{:S(2)}, u32[]{:S(2)}) collective-permute-start(bf16[256,1024]{1,0:T(8,128)(2,1)} %collective-permute-done.4), channel_id=1, source_target_pairs={{0,64},{4,68},{8,72},{12,76},{16,80},{20,84},{24,88},{28,92},{32,9... | collective-permute-start | bytes 1572872 | tf_op jit(solution)/shard_map/ppermute | solution.py:32
  73.0 2.0 copy.85
  75.0 1.6 fusion.25
  76.6 9.0 %collective-permute-done.2 = bf16[256,1024]{0,1:T(8,128)(2,1)} collective-permute-done((bf16[256,1024]{0,1:T(8,128)(2,1)}, bf16[256,1024]{0,1:T(8,128)(2,1)}, u32[]{:S(2)}, u32[]{:S(2)}) %collective-permute-start.2) | collective-permute-done | bytes 524320 | tf_op jit(solution)/shard_map/ppermute | solution.py:32
  85.7 1.6 fusion.27
  87.3 1.5 exponential_reduce_fusion.2
  88.8 1.5 fusion.21
  90.4 1.6 fusion.12
  92.0 4.1 %collective-permute-done.5 = bf16[256,1024]{1,0:T(8,128)(2,1)} collective-permute-done((bf16[256,1024]{1,0:T(8,128)(2,1)}, bf16[256,1024]{1,0:T(8,128)(2,1)}, u32[]{:S(2)}, u32[]{:S(2)}) %collective-permute-start.5) | collective-permute-done | bytes 524320 | tf_op jit(solution)/shard_map/ppermute | solution.py:32
  96.0 2.0 copy.83
  98.1 2.6 %convolution_add_fusion.3 = f32[8,256,128]{1,2,0:T(8,128)S(1)} fusion(f32[8,256,128]{1,2,0:T(8,128)} %fusion.12, bf16[256,8,128]{0,2,1:T(8,128)(2,1)} %bitcast.160, f32[8,256,256]{1,2,0:T(8,128)} %copy-done, f32[8,256]{1,0:T(8,128)S(1)} %log_add_fusion, pred[8]{0:T(512)(128)(4,1)S(1)} %get-tuple-element.13), kind=kOutput, calls=%fused_computation.27 | convolution fusion | flops 136052736 | bytes 4726792 | tf_op jit(solution)/shard_map/bhij,bjhd->bihd/dot_general | solution.py:108
  107.4 1.4 fusion.30
  110.4 1.5 fusion.28
  111.9 1.4 convolution_convert_fusion
  113.3 1.3 convolution_convert_fusion.5
  114.6 1.4 convolution_add_fusion.1
  117.2 2.2 fusion.8
  119.4 2.0 copy.129
  122.5 1.9 collective-permute-start.8
  124.4 2.1 copy.113
  127.8 2.5 %copy.110 = f32[256,1024]{1,0:T(8,128)} copy(f32[256,1024]{0,1:T(8,128)} %bitcast.154) | data formatting | bytes 2097152 | tf_op jit(solution)/shard_map/reshape | solution.py:42
  130.3 2.1 copy.109
  132.4 1.5 collective-permute-start.6
  135.0 1.9 collective-permute-start.11
  136.9 2.1 convolution_convert_fusion.1
  141.4 2.1 convolution_convert_fusion.2
  145.8 1.5 fusion.10
  147.3 1.6 copy.122
  149.0 8.4 %collective-permute-done.7 = bf16[256,1024]{1,0:T(8,128)(2,1)} collective-permute-done((bf16[256,1024]{1,0:T(8,128)(2,1)}, bf16[256,1024]{1,0:T(8,128)(2,1)}, u32[]{:S(2)}, u32[]{:S(2)}) %collective-permute-start.7) | collective-permute-done | bytes 524320 | tf_op jit(solution)/shard_map/ppermute | solution.py:32
  157.4 45.0 %collective-permute-done.6 = bf16[256,1024]{1,0:T(8,128)(2,1)} collective-permute-done((bf16[256,1024]{1,0:T(8,128)(2,1)}, bf16[256,1024]{1,0:T(8,128)(2,1)}, u32[]{:S(2)}, u32[]{:S(2)}) %collective-permute-start.6) | collective-permute-done | bytes 524320 | tf_op jit(solution)/shard_map/ppermute | solution.py:32
  202.3 2.5 %add_convert_fusion.1 = bf16[256,1024]{1,0:T(8,128)(2,1)} fusion(bf16[256,1024]{1,0:T(8,128)(2,1)} %collective-permute-done.8, bf16[256,1024]{1,0:T(8,128)(2,1)} %collective-permute-done.7, f32[256,1024]{1,0:T(8,128)S(1)} %copy-done.8, bf16[256,1024]{1,0:T(8,128)(2,1)} %collective-permute-done.6), kind=kLoop, calls=%fused_computation.38 | loop fusion | flops 1835008 | bytes 3145728 | tf_op jit(solution)/shard_map/convert_element_type | solution.py:154
  204.8 39.0 %collective-permute-done.9 = bf16[256,1024]{1,0:T(8,128)(2,1)S(1)} collective-permute-done((bf16[256,1024]{1,0:T(8,128)(2,1)}, bf16[256,1024]{1,0:T(8,128)(2,1)S(1)}, u32[]{:S(2)}, u32[]{:S(2)}) %collective-permute-start.9) | collective-permute-done | bytes 524320 | tf_op jit(solution)/shard_map/ppermute | solution.py:32
  243.9 2.3 add_convert_fusion
  (74 shorter events, 23.4 us)
Async XLA Ops:
  1.9 17.8 %copy-start.6 = (bf16[256,1024]{0,1:T(8,128)(2,1)}, bf16[256,1024]{0,1:T(8,128)(2,1)S(1)}, u32[]{:S(2)}) copy-start(bf16[256,1024]{0,1:T(8,128)(2,1)S(1)} %copy.157) | copy-start | bytes 1572868
  1.9 18.3 %collective-permute-start = (bf16[256,1024]{0,1:T(8,128)(2,1)S(1)}, bf16[256,1024]{0,1:T(8,128)(2,1)}, u32[]{:S(2)}, u32[]{:S(2)}) collective-permute-start(bf16[256,1024]{0,1:T(8,128)(2,1)S(1)} %copy.157), channel_id=1, source_target_pairs={{0,32},{4,36},{8,40},{12,44},{16,48},{20,52},{24,56},{28,60},{32,6... | collective-permute-start | bytes 1572872 | tf_op jit(solution)/shard_map/ppermute | solution.py:32
  6.8 12.0 %copy-start.19 = (bf16[256,1024]{1,0:T(8,128)(2,1)S(1)}, bf16[256,1024]{1,0:T(8,128)(2,1)}, u32[]{:S(2)}) copy-start(bf16[256,1024]{1,0:T(8,128)(2,1)} %param.7) | copy-start | bytes 1572868
  7.9 11.2 %copy-start.20 = (s32[1,3]{1,0:T(1,128)S(1)}, s32[1,3]{1,0:T(1,128)}, u32[]{:S(2)}) copy-start(s32[1,3]{1,0:T(1,128)} %param.13) | copy-start | bytes 40
  7.9 40.5 %all-to-all-start = ((bf16[4,256,512]{1,2,0:T(8,128)(2,1)}), bf16[4,256,512]{1,2,0:T(8,128)(2,1)}, u32[]{:S(2)}, u32[]{:S(2)}) async-start(bf16[4,256,512]{1,2,0:T(8,128)(2,1)} %broadcast_in_dim.79), calls=%async_computation | async-start | bytes 2097152 | tf_op jit(solution)/shard_map/all_to_all | solution.py:22
  13.0 17.0 %collective-permute-start.3 = (bf16[256,1024]{1,0:T(8,128)(2,1)}, bf16[256,1024]{1,0:T(8,128)(2,1)}, u32[]{:S(2)}, u32[]{:S(2)}) collective-permute-start(bf16[256,1024]{1,0:T(8,128)(2,1)} %param.9), channel_id=1, source_target_pairs={{0,32},{4,36},{8,40},{12,44},{16,48},{20,52},{24,56},{28,60},{32,6... | collective-permute-start | bytes 1572872 | tf_op jit(solution)/shard_map/ppermute | solution.py:32
  18.8 6.5 %copy-start.21 = (s32[8,3]{0,1:T(4,128)S(1)}, s32[8,3]{0,1:T(4,128)}, u32[]{:S(2)}) copy-start(s32[8,3]{0,1:T(4,128)} %param.12) | copy-start | bytes 292
  20.2 20.9 %collective-permute-start.1 = (bf16[256,1024]{0,1:T(8,128)(2,1)}, bf16[256,1024]{0,1:T(8,128)(2,1)}, u32[]{:S(2)}, u32[]{:S(2)}) collective-permute-start(bf16[256,1024]{0,1:T(8,128)(2,1)} %collective-permute-done), channel_id=1, source_target_pairs={{0,32},{4,36},{8,40},{12,44},{16,48},{20,52},{24,56},{28,60},{32,6... | collective-permute-start | bytes 1572872 | tf_op jit(solution)/shard_map/ppermute | solution.py:32
  30.0 38.8 %collective-permute-start.4 = (bf16[256,1024]{1,0:T(8,128)(2,1)}, bf16[256,1024]{1,0:T(8,128)(2,1)}, u32[]{:S(2)}, u32[]{:S(2)}) collective-permute-start(bf16[256,1024]{1,0:T(8,128)(2,1)} %collective-permute-done.3), channel_id=1, source_target_pairs={{0,32},{4,36},{8,40},{12,44},{16,48},{20,52},{24,56},{28,60},{32,6... | collective-permute-start | bytes 1572872 | tf_op jit(solution)/shard_map/ppermute | solution.py:32
  41.2 44.5 %collective-permute-start.2 = (bf16[256,1024]{0,1:T(8,128)(2,1)}, bf16[256,1024]{0,1:T(8,128)(2,1)}, u32[]{:S(2)}, u32[]{:S(2)}) collective-permute-start(bf16[256,1024]{0,1:T(8,128)(2,1)} %collective-permute-done.1), channel_id=1, source_target_pairs={{0,64},{4,68},{8,72},{12,76},{16,80},{20,84},{24,88},{28,92},{32,9... | collective-permute-start | bytes 1572872 | tf_op jit(solution)/shard_map/ppermute | solution.py:32
  68.7 27.3 %collective-permute-start.5 = (bf16[256,1024]{1,0:T(8,128)(2,1)}, bf16[256,1024]{1,0:T(8,128)(2,1)}, u32[]{:S(2)}, u32[]{:S(2)}) collective-permute-start(bf16[256,1024]{1,0:T(8,128)(2,1)} %collective-permute-done.4), channel_id=1, source_target_pairs={{0,64},{4,68},{8,72},{12,76},{16,80},{20,84},{24,88},{28,92},{32,9... | collective-permute-start | bytes 1572872 | tf_op jit(solution)/shard_map/ppermute | solution.py:32
  76.6 12.2 %copy-start.2 = (f32[8,256,256]{1,2,0:T(8,128)}, f32[8,256,256]{1,2,0:T(8,128)S(1)}, u32[]{:S(2)}) copy-start(f32[8,256,256]{1,2,0:T(8,128)S(1)} %get-tuple-element.22) | copy-start | bytes 6291460
  76.6 10.7 %copy-start.4 = (f32[8,256,256]{1,2,0:T(8,128)S(1)}, f32[8,256,256]{1,2,0:T(8,128)}, u32[]{:S(2)}) copy-start(f32[8,256,256]{1,2,0:T(8,128)} %get-tuple-element.20) | copy-start | bytes 6291460
  87.2 1.5 copy-start
  87.3 1.5 copy-start.15
  88.8 1.6 copy-start.11
  98.1 2.7 %copy-start.3 = (f32[8,256,256]{1,2,0:T(8,128)S(1)}, f32[8,256,256]{1,2,0:T(8,128)}, u32[]{:S(2)}) copy-start(f32[8,256,256]{1,2,0:T(8,128)} %copy-done.2) | copy-start | bytes 6291460
  98.1 3.0 %copy-start.9 = (f32[256,1024]{0,1:T(8,128)S(1)}, f32[256,1024]{0,1:T(8,128)}, u32[]{:S(2)}) copy-start(f32[256,1024]{0,1:T(8,128)} %copy.156) | copy-start | bytes 3145732
  98.1 3.3 %copy-start.10 = (f32[8,256,128]{1,2,0:T(8,128)S(1)}, f32[8,256,128]{1,2,0:T(8,128)}, u32[]{:S(2)}) copy-start(f32[8,256,128]{1,2,0:T(8,128)} %fusion.21) | copy-start | bytes 3145732
  98.1 3.4 %copy-start.13 = (bf16[256,1024]{0,1:T(8,128)(2,1)S(1)}, bf16[256,1024]{0,1:T(8,128)(2,1)}, u32[]{:S(2)}) copy-start(bf16[256,1024]{0,1:T(8,128)(2,1)} %copy.85) | copy-start | bytes 1572868
  101.5 1.6 copy-start.5
  101.5 1.7 copy-start.16
  103.2 1.0 copy-start.12
  104.2 1.6 copy-start.1
  104.2 1.7 copy-start.14
  107.4 2.7 %copy-start.7 = (bf16[256,1024]{0,1:T(8,128)(2,1)S(1)}, bf16[256,1024]{0,1:T(8,128)(2,1)}, u32[]{:S(2)}) copy-start(bf16[256,1024]{0,1:T(8,128)(2,1)} %copy-done.6) | copy-start | bytes 1572868
  117.2 4.3 %copy-start.18 = (bf16[8,256,128]{1,2,0:T(8,128)(2,1)S(1)}, bf16[8,256,128]{1,2,0:T(8,128)(2,1)}, u32[]{:S(2)}) copy-start(bf16[8,256,128]{1,2,0:T(8,128)(2,1)} %convolution_convert_fusion.3) | copy-start | bytes 1572868
  122.5 22.1 %collective-permute-start.8 = (bf16[256,1024]{1,0:T(8,128)(2,1)}, bf16[256,1024]{1,0:T(8,128)(2,1)}, u32[]{:S(2)}, u32[]{:S(2)}) collective-permute-start(bf16[256,1024]{1,0:T(8,128)(2,1)} %copy.116), channel_id=1, source_target_pairs={{32,0},{36,4},{40,8},{44,12},{48,16},{52,20},{56,24},{60,28},{64,3... | collective-permute-start | bytes 1572872 | tf_op jit(solution)/shard_map/ppermute | solution.py:32
  124.4 9.6 %copy-start.17 = (bf16[8,128,256]{2,1,0:T(8,128)(2,1)S(1)}, bf16[8,128,256]{2,1,0:T(8,128)(2,1)}, u32[]{:S(2)}) copy-start(bf16[8,128,256]{2,1,0:T(8,128)(2,1)} %convolution_convert_fusion) | copy-start | bytes 1572868
  126.5 30.8 %collective-permute-start.7 = (bf16[256,1024]{1,0:T(8,128)(2,1)}, bf16[256,1024]{1,0:T(8,128)(2,1)}, u32[]{:S(2)}, u32[]{:S(2)}) collective-permute-start(bf16[256,1024]{1,0:T(8,128)(2,1)} %copy.113), channel_id=1, source_target_pairs={{64,0},{68,4},{72,8},{76,12},{80,16},{84,20},{88,24},{92,28},{96,3... | collective-permute-start | bytes 1572872 | tf_op jit(solution)/shard_map/ppermute | solution.py:32
  132.4 69.9 %collective-permute-start.6 = (bf16[256,1024]{1,0:T(8,128)(2,1)}, bf16[256,1024]{1,0:T(8,128)(2,1)}, u32[]{:S(2)}, u32[]{:S(2)}) collective-permute-start(bf16[256,1024]{1,0:T(8,128)(2,1)} %copy.109), channel_id=1, source_target_pairs={{128,0},{132,4},{136,8},{140,12},{144,16},{148,20},{152,24},{156,2... | collective-permute-start | bytes 1572872 | tf_op jit(solution)/shard_map/ppermute | solution.py:32
  135.0 69.8 %collective-permute-start.11 = (bf16[256,1024]{1,0:T(8,128)(2,1)}, bf16[256,1024]{1,0:T(8,128)(2,1)}, u32[]{:S(2)}, u32[]{:S(2)}) collective-permute-start(bf16[256,1024]{1,0:T(8,128)(2,1)} %copy.128), channel_id=1, source_target_pairs={{32,0},{36,4},{40,8},{44,12},{48,16},{52,20},{56,24},{60,28},{64,3... | collective-permute-start | bytes 1572872 | tf_op jit(solution)/shard_map/ppermute | solution.py:32
  140.1 64.8 %collective-permute-start.10 = (bf16[256,1024]{1,0:T(8,128)(2,1)}, bf16[256,1024]{1,0:T(8,128)(2,1)}, u32[]{:S(2)}, u32[]{:S(2)}) collective-permute-start(bf16[256,1024]{1,0:T(8,128)(2,1)} %copy.125), channel_id=1, source_target_pairs={{64,0},{68,4},{72,8},{76,12},{80,16},{84,20},{88,24},{92,28},{96,3... | collective-permute-start | bytes 1572872 | tf_op jit(solution)/shard_map/ppermute | solution.py:32
  144.5 99.3 %collective-permute-start.9 = (bf16[256,1024]{1,0:T(8,128)(2,1)}, bf16[256,1024]{1,0:T(8,128)(2,1)S(1)}, u32[]{:S(2)}, u32[]{:S(2)}) collective-permute-start(bf16[256,1024]{1,0:T(8,128)(2,1)} %copy.121), channel_id=1, source_target_pairs={{128,0},{132,4},{136,8},{140,12},{144,16},{148,20},{152,24},{156,2... | collective-permute-start | bytes 1572872 | tf_op jit(solution)/shard_map/ppermute | solution.py:32
  147.3 55.0 %copy-start.8 = (f32[256,1024]{1,0:T(8,128)S(1)}, f32[256,1024]{1,0:T(8,128)}, u32[]{:S(2)}) copy-start(f32[256,1024]{1,0:T(8,128)} %copy.110) | copy-start | bytes 3145732
where the time goes:
time: 248 us; the launch traced here: 246 us
  waiting for transfers between devices  122 us (49%)
  starting transfers between devices  42.8 us (17%)
  matrix products  38.4 us (15%)
  local copies, waits for them, and re-layouts  33.4 us (13%)
  other arithmetic  8.15 us (3%)
    ppermute x12, waiting for transfers between devices, shifted(): lax.ppermute(value, axis, [(source, source + steps) for source in range(i...  122 us
    ppermute x12, starting transfers between devices, shifted(): lax.ppermute(value, axis, [(source, source + steps) for source in range(i...  37.7 us
    dot_general x4, matrix products, body(): jnp.einsum('bhij,bihd->bjhd', weight_list[set_index], grad_blocks, prefer...  7.15 us
    dot_general x4, matrix products, body(): jnp.einsum('bihd,bjhd->bhij', query_blocks, key_entry[0], preferred_eleme...  6.63 us
    dot_general x4, matrix products, body(): jnp.einsum('bhij,bjhd->bihd', weight_set, key_entry[1], preferred_element...  6.34 us
    unnamed x46, local copies, waits for them, and re-layouts  6.19 us
    ppermute x3, local copies, waits for them, and re-layouts, shifted(): lax.ppermute(value, axis, [(source, source + steps) for source in range(i...  6.12 us
    dot_general x4, matrix products, body(): jnp.einsum('bhij,bihd->bjhd', dlogit, query_blocks, preferred_element_typ...  5.35 us
  transfers between devices with their start and end apart: 13, of which 8 were waited for; matrix products, arithmetic and copies ran while one was open for 20% of the time, Pallas kernels for 0%

commit v1 on v0

v1 whole, which is shorter than its diff:
```python
import functools
import math

import jax
import jax.numpy as jnp
from jax import lax
from jax.experimental import pallas as pl
from jax.experimental.pallas import tpu as pltpu
from jax.sharding import PartitionSpec as P

BLK = 256
HDIM = 128
SECTIONS = 3
LAG = 2
AHEAD = 3
MESH = pl.DeviceIdType.MESH
HIDE = -1e30
SCALE = 1.0 / math.sqrt(HDIM)
NT = (((1,), (1,)), ((), ()))
TN = (((0,), (0,)), ((), ()))
NN = (((1,), (0,)), ((), ()))


def mm(a, b, dims):
    return lax.dot_general(a, b, dims, preferred_element_type=jnp.float32)


def kernel(
    seq_count, head_count, bias, q_in, k_in, v_in, og_in, w_in, dq, dk, dv,
    qa, ga, ka, va, og, w, scores, slopes, own_dk, own_dv, sent, got,
    local_sem, og_send, og_recv, bulk_send, bulk_recv, row_send, row_recv,
):
    heads = q_in.shape[1] // HDIM
    seq = lax.axis_index("seq")
    me = lax.axis_index("head")
    stride = seq_count // 8

    def along(steps):
        return {"seq": lax.rem(seq + (steps % 8) * stride, seq_count)}

    def peer(offset):
        return {"head": lax.rem(me + offset, head_count)}

    def cols(h):
        return pl.ds(pl.multiple_of(h * HDIM, HDIM), HDIM)

    bulk = {"k": (ka, 0, 1), "v": (va, 1, 1), "q": (qa, 2, -1), "g": (ga, 3, -1)}

    def move(kind, hop, h):
        ref, row, sign = bulk[kind]
        return pltpu.make_async_remote_copy(
            src_ref=ref.at[hop, :, cols(h)],
            dst_ref=ref.at[hop + 1, :, cols(h)],
            send_sem=bulk_send.at[row, hop, h],
            recv_sem=bulk_recv.at[row, hop, h],
            device_id=along(sign * (2 if hop == 2 else 1)),
            device_id_type=MESH,
        )

    def rows_move(hop, h):
        return pltpu.make_async_remote_copy(
            src_ref=sent.at[hop, h],
            dst_ref=got.at[hop, h],
            send_sem=row_send.at[hop, h],
            recv_sem=row_recv.at[hop, h],
            device_id=along(-(1, 2, 4)[hop]),
            device_id_type=MESH,
        )

    def og_move(offset):
        return pltpu.make_async_remote_copy(
            src_ref=og.at[0],
            dst_ref=og.at[head_count - offset],
            send_sem=og_send.at[offset - 1],
            recv_sem=og_recv.at[head_count - offset - 1],
            device_id=peer(offset),
            device_id_type=MESH,
        )

    locals_ = [
        pltpu.make_async_copy(source, target, local_sem.at[index])
        for index, (source, target) in enumerate(
            ((k_in, ka.at[0]), (v_in, va.at[0]), (q_in, qa.at[0]), (og_in, og.at[0]), (w_in, w))
        )
    ]
    for copy in locals_:
        copy.start()

    barrier = pltpu.get_barrier_semaphore()
    for steps in (1, -1, 2, -2, 4):
        pl.semaphore_signal(barrier, inc=1, device_id=along(steps), device_id_type=MESH)
    for offset in range(1, head_count):
        pl.semaphore_signal(barrier, inc=1, device_id=peer(offset), device_id_type=MESH)
    pl.semaphore_wait(barrier, 5 + head_count - 1)

    for copy in locals_[:4]:
        copy.wait()
    for offset in range(1, head_count):
        og_move(offset).start()

    @pl.loop(0, heads)
    def _(h):
        for kind in "kvq":
            move(kind, 0, h).start()

    locals_[4].wait()
    for offset in range(1, head_count):
        og_move(head_count - offset).wait_recv()
    width = og.shape[2]

    @pl.loop(0, heads // 2)
    def _(pair):
        wide = pl.ds(pl.multiple_of(pair * 2 * HDIM, 2 * HDIM), 2 * HDIM)
        total = jnp.zeros((BLK, 2 * HDIM), jnp.float32)
        for offset in range(head_count):
            owner = lax.rem(me + offset, head_count)
            features = pl.ds(pl.multiple_of(owner * width, width), width)
            total = total + mm(og[offset], w[wide, features], NT)
        ga[0, :, wide] = total.astype(jnp.bfloat16)

    @pl.loop(0, heads)
    def _(h):
        move("g", 0, h).start()

    @pl.loop(0, heads)
    def _(h):
        for kind in "kvq":
            move(kind, 0, h).wait_recv()
            move(kind, 1, h).start()

    @pl.loop(0, heads)
    def _(h):
        move("g", 0, h).wait_recv()
        move("g", 1, h).start()

    @pl.loop(0, heads)
    def _(h):
        for kind in "kv":
            move(kind, 1, h).wait_recv()
            move(kind, 2, h).start()
        for kind in "qg":
            move(kind, 1, h).wait_recv()

        @pl.when(h < AHEAD)
        def _():
            for kind in "qg":
                move(kind, 2, h).start()

    def query_side(h):
        at = cols(h)
        query = qa[0, :, at]
        grad = ga[0, :, at]
        key_index = lax.broadcasted_iota(jnp.int32, (BLK, BLK), 0)
        query_index = lax.broadcasted_iota(jnp.int32, (BLK, BLK), 1)
        top = None
        for s in range(SECTIONS + 1):
            raw = mm(ka[s, :, at], query, NT) * SCALE
            if s == 0:
                raw = jnp.where(key_index <= query_index, raw, HIDE)
            else:
                raw = raw + bias[(SECTIONS - s) * heads + h]
            scores[s] = raw
            high = jnp.max(raw, axis=0, keepdims=True)
            top = high if top is None else jnp.maximum(top, high)
        total = None
        for s in range(SECTIONS + 1):
            part = jnp.exp(scores[s] - top)
            scores[s] = part
            part = jnp.sum(part, axis=0, keepdims=True)
            total = part if total is None else total + part
        inverse = 1.0 / total
        delta = None
        for s in range(SECTIONS + 1):
            probs = scores[s] * inverse
            scores[s] = probs
            weights = probs.astype(jnp.bfloat16)
            slope = mm(va[s, :, at], grad, NT)
            slopes[s] = slope
            part = jnp.sum(weights.astype(jnp.float32) * slope, axis=0, keepdims=True)
            delta = part if delta is None else delta + part
            if s == 0:
                own_dv[:, at] = mm(weights, grad, NN)
        log_norm = top + jnp.log(total)
        for hop in range(SECTIONS):
            sent[hop, h, 0:1, :] = log_norm - bias[(SECTIONS - 1 - hop) * heads + h]
            sent[hop, h, 1:2, :] = delta
        query_sum = None
        for s in range(SECTIONS + 1):
            dlogit = (scores[s] * (slopes[s] - delta) * SCALE).astype(jnp.bfloat16)
            part = mm(dlogit, ka[s, :, at], TN)
            query_sum = part if query_sum is None else query_sum + part
            if s == 0:
                own_dk[:, at] = mm(dlogit, query, NN)
        dq[:, at] = query_sum.astype(jnp.bfloat16)

    def key_side(h):
        at = cols(h)
        key = ka[0, :, at]
        value = va[0, :, at]
        key_sum = own_dk[:, at]
        value_sum = own_dv[:, at]
        for hop in range(SECTIONS):
            query = qa[hop + 1, :, at]
            grad = ga[hop + 1, :, at]
            log_norm = got[hop, h, 0:1, :]
            delta = got[hop, h, 1:2, :]
            probs = jnp.exp(mm(key, query, NT) * SCALE - log_norm)
            slope = mm(value, grad, NT)
            dlogit = (probs * (slope - delta) * SCALE).astype(jnp.bfloat16)
            key_sum = key_sum + mm(dlogit, query, NN)
            value_sum = value_sum + mm(probs.astype(jnp.bfloat16), grad, NN)
        dk[:, at] = key_sum.astype(jnp.bfloat16)
        dv[:, at] = value_sum.astype(jnp.bfloat16)

    @pl.loop(0, heads + LAG)
    def _(step):
        @pl.when(step + AHEAD < heads)
        def _():
            for kind in "qg":
                move(kind, 2, step + AHEAD).start()

        @pl.when(step < heads)
        def _():
            for kind in "kv":
                move(kind, 2, step).wait_recv()
            query_side(step)
            for hop in range(SECTIONS):
                rows_move(hop, step).start()

        @pl.when(step >= LAG)
        def _():
            h = step - LAG
            for kind in "qg":
                move(kind, 2, h).wait_recv()
            for hop in range(SECTIONS):
                rows_move(hop, h).wait_recv()
            key_side(h)

    @pl.loop(0, heads)
    def _(h):
        for hop in range(SECTIONS):
            rows_move(hop, h).wait_send()
            for kind in "kvqg":
                move(kind, hop, h).wait_send()

    for offset in range(1, head_count):
        og_move(offset).wait_send()


def body(queries, key_rows, value_rows, out_grad, out_proj, section_table, block_active):
    seq_count = lax.axis_size("seq")
    head_count = lax.axis_size("head")
    heads = queries.shape[1] // HDIM
    position = lax.axis_index("seq")
    spans = jnp.array([seq_count // 2 ** (index + 1) for index in range(SECTIONS)], jnp.int32)
    usable = (section_table.T * block_active[0][:, None] > 0) & (position >= spans)[:, None]
    bias = jnp.where(usable, 0.0, HIDE).astype(jnp.float32).reshape(SECTIONS * heads)
    width = queries.shape[1]
    four = (SECTIONS + 1, BLK, width)
    any_space = pl.BlockSpec(memory_space=pl.ANY)
    vmem = pl.BlockSpec(memory_space=pltpu.VMEM)
    out = jax.ShapeDtypeStruct((BLK, width), jnp.bfloat16)
    return pl.pallas_call(
        functools.partial(kernel, seq_count, head_count),
        out_shape=(out, out, out),
        in_specs=[pl.BlockSpec(memory_space=pltpu.SMEM)] + [any_space] * 5,
        out_specs=(vmem, vmem, vmem),
        scratch_shapes=[
            pltpu.VMEM(four, jnp.bfloat16),
            pltpu.VMEM(four, jnp.bfloat16),
            pltpu.VMEM(four, jnp.bfloat16),
            pltpu.VMEM(four, jnp.bfloat16),
            pltpu.VMEM((head_count, *out_grad.shape), jnp.bfloat16),
            pltpu.VMEM(out_proj.shape, jnp.bfloat16),
            pltpu.VMEM((SECTIONS + 1, BLK, BLK), jnp.float32),
            pltpu.VMEM((SECTIONS + 1, BLK, BLK), jnp.float32),
            pltpu.VMEM((BLK, width), jnp.float32),
            pltpu.VMEM((BLK, width), jnp.float32),
            pltpu.VMEM((SECTIONS, heads, 2, BLK), jnp.float32),
            pltpu.VMEM((SECTIONS, heads, 2, BLK), jnp.float32),
            pltpu.SemaphoreType.DMA((5,)),
            pltpu.SemaphoreType.DMA((head_count - 1,)),
            pltpu.SemaphoreType.DMA((head_count - 1,)),
            pltpu.SemaphoreType.DMA((4, SECTIONS, heads)),
            pltpu.SemaphoreType.DMA((4, SECTIONS, heads)),
            pltpu.SemaphoreType.DMA((SECTIONS, heads)),
            pltpu.SemaphoreType.DMA((SECTIONS, heads)),
        ],
        compiler_params=pltpu.CompilerParams(
            collective_id=0, has_side_effects=True, vmem_limit_bytes=60 * 1024 * 1024
        ),
        name="attention_grads",
    )(bias, queries, key_rows, value_rows, out_grad, out_proj)


def solution(mesh):
    return jax.shard_map(
        body,
        mesh=mesh,
        in_specs=(
            P("seq", "head"),
            P("seq", "head"),
            P("seq", "head"),
            P("seq", "head"),
            P("head", None),
            P("head", None),
            P("seq", None),
        ),
        out_specs=(P("seq", "head"), P("seq", "head"), P("seq", "head")),
        check_vma=False,
    )
```

time: 248 us -> 130 us (0.52)
  the two profiles are of different devices: /device:TPU:60 before, /device:TPU:30 now
where the time goes in v1:
time: 130 us; the launch traced here: 129 us
  Pallas kernels  121 us (93%)
  local copies, waits for them, and re-layouts  6.2 us (5%)
  other arithmetic  1.42 us (1%)
    pallas_call x1, Pallas kernels, body(): pl.pallas_call(functools.partial(kernel, seq_count, head_count), out_shap...  121 us
    unnamed x3, local copies, waits for them, and re-layouts  5.6 us

profile of v1, /device:TPU:30, one launch (start us, length us, event | category | flops | bytes accessed | tf_op | source)
XLA Modules:
  0.0 129.5 jit_solution(17364808186218360733)
XLA Ops:
  0.6 0.7 broadcast_compare_fusion
  1.3 0.8 select_bitcast_fusion
  2.1 0.6 reshape.11.bias
  2.6 121.2 %attention_grads.1 = (bf16[256,1024]{1,0:T(8,128)(2,1)}, bf16[256,1024]{1,0:T(8,128)(2,1)}, bf16[256,1024]{1,0:T(8,128)(2,1)}) custom-call(f32[24]{0:T(128)} %reshape.11.bias, bf16[256,1024]{1,0:T(8,128)(2,1)} %q_in.1, bf16[256,1024]{1,0:T(8,128)(2,1)} %k_in.1, bf16[256,1024]{1,0:T(8,128)(2,1)} %v_in.1, bf16[256,512]{1,0:T(8,128)(2,1)} %og_in.1, ...), custom_call_target="tpu_custom_call" | custom-call | tf_op jit(solution)/shard_map/attention_grads/pallas_call | solution.py:263
  123.9 1.9 %copy.14 = bf16[256,1024]{1,0:T(8,128)(2,1)} copy(bf16[256,1024]{1,0:T(8,128)(2,1)} %get-tuple-element.6) | data formatting | bytes 1048576
  125.8 1.9 %copy.15 = bf16[256,1024]{1,0:T(8,128)(2,1)} copy(bf16[256,1024]{1,0:T(8,128)(2,1)} %get-tuple-element.7) | data formatting | bytes 1048576
  127.6 1.9 %copy.16 = bf16[256,1024]{1,0:T(8,128)(2,1)} copy(bf16[256,1024]{1,0:T(8,128)(2,1)} %get-tuple-element.8) | data formatting | bytes 1048576

commit v2 on v1

v2 whole, which is shorter than its diff:
```python
import functools
import math

import jax
import jax.numpy as jnp
from jax import lax
from jax.experimental import pallas as pl
from jax.experimental.pallas import tpu as pltpu
from jax.sharding import PartitionSpec as P

BLK = 256
HDIM = 128
SECTIONS = 3
MESH = pl.DeviceIdType.MESH
HIDE = -1e30
SCALE = 1.0 / math.sqrt(HDIM)
NT = (((1,), (1,)), ((), ()))
TN = (((0,), (0,)), ((), ()))
NN = (((1,), (0,)), ((), ()))


def mm(a, b, dims):
    return lax.dot_general(a, b, dims, preferred_element_type=jnp.float32)


def kernel(
    seq_count, moved, table, active, q_in, k_in, v_in, og_in, w_in, dq, dk, dv,
    qa, ga, ka, va, og, w, scores, slopes, held_p, held_s, tops, norms, own_dk, own_dv, parts,
    stat_out, stat_in, row_out, row_in, back_out, back_in,
    local_sem, og_send, og_recv, near_send, near_recv, bulk_send, bulk_recv,
    stat_send, stat_recv, row_send, row_recv, back_send, back_recv,
):
    heads = q_in.shape[1] // HDIM
    width = og_in.shape[1]
    seq = lax.axis_index("seq")
    me = lax.axis_index("head")
    stride = seq_count // 8
    mates = (me, me + 1 - 2 * (me % 2), me + 2 - 4 * (me // 2), 3 - me)

    def along(steps):
        return {"seq": lax.rem(seq + (steps % 8) * stride, seq_count)}

    def cols(h):
        return pl.ds(pl.multiple_of(h * HDIM, HDIM), HDIM)

    def remote(source, target, send, recv, device):
        return pltpu.make_async_remote_copy(
            src_ref=source, dst_ref=target, send_sem=send, recv_sem=recv,
            device_id=device, device_id_type=MESH,
        )

    bulk = {"k": (ka, 0, 1), "v": (va, 1, 1), "q": (qa, 2, -1)}

    def move(kind, hop, h):
        ref, row, sign = bulk[kind]
        return remote(
            ref.at[hop, :, cols(h)], ref.at[hop + 1, :, cols(h)],
            bulk_send.at[row, hop, h], bulk_recv.at[row, hop, h],
            along(sign * (2 if hop == 2 else 1)),
        )

    def og_move(hop):
        return remote(
            og.at[hop, 0], og.at[hop + 1, 0], og_send.at[hop], og_recv.at[hop],
            along(-(2 if hop == 2 else 1)),
        )

    def near(slot, which):
        source, target, mate = ((0, 1, 1), (0, 2, 2), (2, 3, 1))[which]
        return remote(
            og.at[slot, source], og.at[slot, target], near_send.at[slot, which],
            near_recv.at[slot, which], {"head": mates[mate]},
        )

    def stat_move(hop, h):
        return remote(
            stat_out.at[hop, h], stat_in.at[hop, h], stat_send.at[hop, h], stat_recv.at[hop, h],
            along((1, 2, 4)[hop]),
        )

    def row_move(hop, h):
        return remote(
            row_out.at[hop, h], row_in.at[hop, h], row_send.at[hop, h], row_recv.at[hop, h],
            along(-(1, 2, 4)[hop]),
        )

    def back_move(hop, h):
        return remote(
            back_out.at[hop, :, cols(h)], back_in.at[hop, :, cols(h)],
            back_send.at[hop, h], back_recv.at[hop, h], along((2, 1, 1)[hop]),
        )

    def hidden(hop, h):
        index = SECTIONS - 1 - hop
        inside = (seq >= seq_count // 2 ** (index + 1)).astype(jnp.int32)
        usable = table[index, h] * active[0, index] * inside
        return (1.0 - usable.astype(jnp.float32)) * HIDE

    def causal(raw):
        key_index = lax.broadcasted_iota(jnp.int32, (BLK, BLK), 0)
        query_index = lax.broadcasted_iota(jnp.int32, (BLK, BLK), 1)
        return jnp.where(key_index <= query_index, raw, HIDE)

    def make_grad(slot):
        near(slot, 0).wait_recv()
        near(slot, 2).wait_recv()

        @pl.loop(0, heads // 2)
        def _(pair):
            wide = pl.ds(pl.multiple_of(pair * 2 * HDIM, 2 * HDIM), 2 * HDIM)
            total = jnp.zeros((BLK, 2 * HDIM), jnp.float32)
            for index, owner in enumerate(mates):
                features = pl.ds(pl.multiple_of(owner * width, width), width)
                total = total + mm(og[slot, index], w[wide, features], NT)
            ga[slot, :, wide] = total.astype(jnp.bfloat16)

    def pass_near(slot):
        near(slot, 1).wait_recv()
        near(slot, 2).start()

    def query_side(h):
        at = cols(h)
        query = qa[0, :, at]
        grad = ga[0, :, at]
        top = None
        for s in range(SECTIONS + 1):
            raw = mm(ka[s, :, at], query, NT) * SCALE
            raw = causal(raw) if s == 0 else raw + hidden(s - 1, h)
            scores[s] = raw
            high = jnp.max(raw, axis=0, keepdims=True)
            top = high if top is None else jnp.maximum(top, high)
        total = None
        for s in range(SECTIONS + 1):
            part = jnp.exp(scores[s] - top)
            scores[s] = part
            part = jnp.sum(part, axis=0, keepdims=True)
            total = part if total is None else total + part
        inverse = 1.0 / total
        delta = None
        for s in range(SECTIONS + 1):
            probs = scores[s] * inverse
            scores[s] = probs
            weights = probs.astype(jnp.bfloat16)
            slope = mm(va[s, :, at], grad, NT)
            slopes[s] = slope
            part = jnp.sum(weights.astype(jnp.float32) * slope, axis=0, keepdims=True)
            delta = part if delta is None else delta + part
            if s == 0:
                own_dv[:, at] = mm(weights, grad, NN)
        log_norm = top + jnp.log(total)
        for hop in range(SECTIONS):
            row_out[hop, h, 0:1, :] = log_norm - hidden(hop, h)
            row_out[hop, h, 1:2, :] = delta
        query_sum = None
        for s in range(SECTIONS + 1):
            dlogit = (scores[s] * (slopes[s] - delta) * SCALE).astype(jnp.bfloat16)
            part = mm(dlogit, ka[s, :, at], TN)
            query_sum = part if query_sum is None else query_sum + part
            if s == 0:
                own_dk[:, at] = mm(dlogit, query, NN)
        dq[:, at] = query_sum.astype(jnp.bfloat16)
        for hop in range(SECTIONS):
            row_move(hop, h).start()

    def key_side(h):
        at = cols(h)
        key = ka[0, :, at]
        value = va[0, :, at]
        key_sum = own_dk[:, at]
        value_sum = own_dv[:, at]
        for hop in range(SECTIONS):
            query = qa[hop + 1, :, at]
            grad = ga[hop + 1, :, at]
            log_norm = row_in[hop, h, 0:1, :]
            delta = row_in[hop, h, 1:2, :]
            probs = jnp.exp(mm(key, query, NT) * SCALE - log_norm)
            slope = mm(value, grad, NT)
            dlogit = (probs * (slope - delta) * SCALE).astype(jnp.bfloat16)
            key_sum = key_sum + mm(dlogit, query, NN)
            value_sum = value_sum + mm(probs.astype(jnp.bfloat16), grad, NN)
        dk[:, at] = key_sum.astype(jnp.bfloat16)
        dv[:, at] = value_sum.astype(jnp.bfloat16)

    def partial_scores(slot, h):
        at = cols(h)
        raw = mm(ka[0, :, at], qa[slot, :, at], NT) * SCALE
        if slot == 0:
            raw = causal(raw)
        top = jnp.max(raw, axis=0, keepdims=True)
        part = jnp.exp(raw - top)
        slope = mm(va[0, :, at], ga[slot, :, at], NT)
        held_p[slot, h] = part
        held_s[slot, h] = slope
        total = jnp.sum(part, axis=0, keepdims=True)
        drift = jnp.sum(part * slope, axis=0, keepdims=True)
        tops[slot, h, 0:1, :] = top
        return top, total, drift

    def stage_own(h):
        top, total, drift = partial_scores(0, h)
        norms[h, 0:1, :] = total
        norms[h, 1:2, :] = drift

    def stage_a(h):
        for kind in ("q",):
            move(kind, 2, h).wait_recv()
        for hop in range(SECTIONS):
            top, total, drift = partial_scores(hop + 1, h)
            stat_out[hop, h, 0:1, :] = top
            stat_out[hop, h, 1:2, :] = total
            stat_out[hop, h, 2:3, :] = drift
            stat_out[hop, h, 3:4, :] = drift
            stat_move(hop, h).start()

    def stage_b(h):
        for hop in range(SECTIONS):
            stat_move(hop, h).wait_recv()
        tops_of = [tops[0, h, 0:1, :]] + [
            stat_in[hop, h, 0:1, :] + hidden(hop, h) for hop in range(SECTIONS)
        ]
        top = functools.reduce(jnp.maximum, tops_of)
        factor = jnp.exp(tops_of[0] - top)
        total = factor * norms[h, 0:1, :]
        drift = factor * norms[h, 1:2, :]
        for hop in range(SECTIONS):
            factor = jnp.exp(tops_of[hop + 1] - top)
            total = total + factor * stat_in[hop, h, 1:2, :]
            drift = drift + factor * stat_in[hop, h, 2:3, :]
        log_norm = top + jnp.log(total)
        delta = drift / total
        norms[h, 0:1, :] = log_norm
        norms[h, 1:2, :] = delta
        for hop in range(SECTIONS):
            row_out[hop, h, 0:1, :] = log_norm - hidden(hop, h)
            row_out[hop, h, 1:2, :] = delta
            row_move(hop, h).start()

    def stage_c(h):
        at = cols(h)
        for hop in range(SECTIONS):
            row_move(hop, h).wait_recv()
        key_sum = None
        value_sum = None
        for slot in (3, 2, 1, 0):
            if slot == 0:
                log_norm, delta = norms[h, 0:1, :], norms[h, 1:2, :]
            else:
                log_norm, delta = row_in[slot - 1, h, 0:1, :], row_in[slot - 1, h, 1:2, :]
            probs = held_p[slot, h] * jnp.exp(tops[slot, h, 0:1, :] - log_norm)
            dlogit = (probs * (held_s[slot, h] - delta) * SCALE).astype(jnp.bfloat16)
            query_part = mm(dlogit, ka[0, :, at], TN)
            if slot == 3:
                back_out[0, :, at] = query_part.astype(jnp.bfloat16)
            else:
                parts[slot, :, at] = query_part
            key_part = mm(dlogit, qa[slot, :, at], NN)
            value_part = mm(probs.astype(jnp.bfloat16), ga[slot, :, at], NN)
            key_sum = key_part if key_sum is None else key_sum + key_part
            value_sum = value_part if value_sum is None else value_sum + value_part
        dk[:, at] = key_sum.astype(jnp.bfloat16)
        dv[:, at] = value_sum.astype(jnp.bfloat16)
        back_move(0, h).start()

    def stage_back(hop, h):
        at = cols(h)
        back_move(hop, h).wait_recv()
        total = (parts[2 - hop, :, at] + back_in[hop, :, at].astype(jnp.float32)).astype(jnp.bfloat16)
        if hop == 2:
            dq[:, at] = total
        else:
            back_out[hop + 1, :, at] = total
            back_move(hop + 1, h).start()

    copies = [
        pltpu.make_async_copy(source, target, local_sem.at[index])
        for index, (source, target) in enumerate(
            ((og_in, og.at[0, 0]), (q_in, qa.at[0]), (k_in, ka.at[0]), (v_in, va.at[0]), (w_in, w))
        )
    ]
    for copy in copies:
        copy.start()

    barrier = pltpu.get_barrier_semaphore()
    for steps in (1, -1, 2, -2, 4):
        pl.semaphore_signal(barrier, inc=1, device_id=along(steps), device_id_type=MESH)
    for mate in mates[1:3]:
        pl.semaphore_signal(barrier, inc=1, device_id={"head": mate}, device_id_type=MESH)
    pl.semaphore_wait(barrier, 7)

    def each(first, last):
        return pl.loop(first, last)

    copies[0].wait()
    og_move(0).start()
    near(0, 1).start()
    near(0, 0).start()
    copies[1].wait()

    @each(0, 2)
    def _(h):
        move("q", 0, h).start()

    copies[2].wait()
    copies[3].wait()

    @each(moved, heads)
    def _(h):
        move("k", 0, h).start()
        move("v", 0, h).start()

    og_move(0).wait_recv()
    og_move(1).start()
    near(1, 1).start()
    near(1, 0).start()

    @each(2, 4)
    def _(h):
        move("q", 0, h).start()

    pass_near(0)

    @each(0, 2)
    def _(h):
        move("q", 0, h).wait_recv()
        move("q", 1, h).start()

    @each(moved, heads)
    def _(h):
        for kind in "kv":
            move(kind, 0, h).wait_recv()
            move(kind, 1, h).start()

    og_move(1).wait_recv()
    og_move(2).start()
    near(2, 1).start()
    near(2, 0).start()

    @each(4, heads)
    def _(h):
        move("q", 0, h).start()

    pass_near(1)

    @each(2, heads)
    def _(h):
        move("q", 0, h).wait_recv()
        move("q", 1, h).start()

    copies[4].wait()
    make_grad(0)

    @each(moved, heads)
    def _(h):
        for kind in "kv":
            move(kind, 1, h).wait_recv()
            move(kind, 2, h).start()

    @each(0, 4)
    def _(h):
        move("q", 1, h).wait_recv()
        move("q", 2, h).start()

    pass_near(2)
    og_move(2).wait_recv()
    near(3, 1).start()
    near(3, 0).start()

    make_grad(1)
    make_grad(2)

    @each(4, heads)
    def _(h):
        move("q", 1, h).wait_recv()

    @each(0, moved)
    def _(h):
        stage_own(h)

    pass_near(3)

    @each(moved, heads - 2)
    def _(h):
        for kind in "kv":
            move(kind, 2, h).wait_recv()
        query_side(h)

    make_grad(3)

    @each(heads - 2, heads)
    def _(h):
        for kind in "kv":
            move(kind, 2, h).wait_recv()
        query_side(h)

    lag_b, lag_c, lag_d, lag_e, lag_f = 2, 3, 5, 7, 9
    lead = 3

    @each(0, moved + lag_f)
    def _(step):
        def when(low, high, action):
            @pl.when((step >= low) & (step < high))
            def _():
                action(step - low)

        when(1, 1 + heads - 4, lambda i: move("q", 2, i + 4).start())
        when(0, moved, stage_a)
        when(lag_b, lag_b + moved, stage_b)
        when(lag_c, lag_c + moved, stage_c)
        when(lag_d, lag_d + moved, lambda i: stage_back(0, i))
        when(lag_e, lag_e + moved, lambda i: stage_back(1, i))
        when(lag_f, lag_f + moved, lambda i: stage_back(2, i))

        def last_heads(i):
            h = i + moved
            move("q", 2, h).wait_recv()
            for hop in range(SECTIONS):
                row_move(hop, h).wait_recv()
            key_side(h)

        when(moved + lead, heads + lead, last_heads)

    @each(0, heads)
    def _(h):
        for hop in range(SECTIONS):
            row_move(hop, h).wait_send()
            move("q", hop, h).wait_send()

    @each(0, moved)
    def _(h):
        for hop in range(SECTIONS):
            stat_move(hop, h).wait_send()
            back_move(hop, h).wait_send()

    @each(moved, heads)
    def _(h):
        for hop in range(SECTIONS):
            for kind in "kv":
                move(kind, hop, h).wait_send()

    for hop in range(SECTIONS):
        og_move(hop).wait_send()
    for slot in range(SECTIONS + 1):
        for which in range(3):
            near(slot, which).wait_send()


def body(queries, key_rows, value_rows, out_grad, out_proj, section_table, block_active):
    seq_count = lax.axis_size("seq")
    heads = queries.shape[1] // HDIM
    moved = heads // 2
    width = queries.shape[1]
    part = moved * HDIM
    four = (SECTIONS + 1, BLK, width)
    any_space = pl.BlockSpec(memory_space=pl.ANY)
    vmem = pl.BlockSpec(memory_space=pltpu.VMEM)
    smem = pl.BlockSpec(memory_space=pltpu.SMEM)
    out = jax.ShapeDtypeStruct((BLK, width), jnp.bfloat16)
    bf16, f32, dma = jnp.bfloat16, jnp.float32, pltpu.SemaphoreType.DMA
    return pl.pallas_call(
        functools.partial(kernel, seq_count, moved),
        out_shape=(out, out, out),
        in_specs=[smem, smem] + [any_space] * 5,
        out_specs=(vmem, vmem, vmem),
        scratch_shapes=[
            pltpu.VMEM(four, bf16),
            pltpu.VMEM(four, bf16),
            pltpu.VMEM(four, bf16),
            pltpu.VMEM(four, bf16),
            pltpu.VMEM((SECTIONS + 1, 4, *out_grad.shape), bf16),
            pltpu.VMEM(out_proj.shape, bf16),
            pltpu.VMEM((SECTIONS + 1, BLK, BLK), f32),
            pltpu.VMEM((SECTIONS + 1, BLK, BLK), f32),
            pltpu.VMEM((SECTIONS + 1, moved, BLK, BLK), f32),
            pltpu.VMEM((SECTIONS + 1, moved, BLK, BLK), f32),
            pltpu.VMEM((SECTIONS + 1, moved, 8, BLK), f32),
            pltpu.VMEM((moved, 8, BLK), f32),
            pltpu.VMEM((BLK, width), f32),
            pltpu.VMEM((BLK, width), f32),
            pltpu.VMEM((SECTIONS, BLK, part), f32),
            pltpu.VMEM((SECTIONS, moved, 4, BLK), f32),
            pltpu.VMEM((SECTIONS, moved, 4, BLK), f32),
            pltpu.VMEM((SECTIONS, heads, 2, BLK), f32),
            pltpu.VMEM((SECTIONS, heads, 2, BLK), f32),
            pltpu.VMEM((SECTIONS, BLK, part), bf16),
            pltpu.VMEM((SECTIONS, BLK, part), bf16),
            dma((5,)),
            dma((SECTIONS,)),
            dma((SECTIONS,)),
            dma((SECTIONS + 1, 3)),
            dma((SECTIONS + 1, 3)),
            dma((3, SECTIONS, heads)),
            dma((3, SECTIONS, heads)),
            dma((SECTIONS, moved)),
            dma((SECTIONS, moved)),
            dma((SECTIONS, heads)),
            dma((SECTIONS, heads)),
            dma((SECTIONS, moved)),
            dma((SECTIONS, moved)),
        ],
        compiler_params=pltpu.CompilerParams(
            collective_id=0, has_side_effects=True, vmem_limit_bytes=60 * 1024 * 1024
        ),
        name="attention_grads",
    )(section_table.T, block_active, queries, key_rows, value_rows, out_grad, out_proj)


def solution(mesh):
    return jax.shard_map(
        body,
        mesh=mesh,
        in_specs=(
            P("seq", "head"),
            P("seq", "head"),
            P("seq", "head"),
            P("seq", "head"),
            P("head", None),
            P("head", None),
            P("seq", None),
        ),
        out_specs=(P("seq", "head"), P("seq", "head"), P("seq", "head")),
        check_vma=False,
    )
```

time: 130 us -> 118 us (0.908)
  the two profiles are of different devices: /device:TPU:30 before, /device:TPU:60 now
where the time goes in v2:
time: 118 us; the launch traced here: 117 us
  Pallas kernels  111 us (94%)
  local copies, waits for them, and re-layouts  5.6 us (5%)
    pallas_call x1, Pallas kernels, body(): pl.pallas_call(functools.partial(kernel, seq_count, moved), out_shape=(ou...  111 us
    unnamed x3, local copies, waits for them, and re-layouts  5.6 us

profile of v2, /device:TPU:60, one launch (start us, length us, event | category | flops | bytes accessed | tf_op | source)
XLA Modules:
  0.0 117.4 jit_solution(5593742150866483953)
XLA Ops:
  0.6 111.1 %attention_grads.1 = (bf16[256,1024]{1,0:T(8,128)(2,1)}, bf16[256,1024]{1,0:T(8,128)(2,1)}, bf16[256,1024]{1,0:T(8,128)(2,1)}) custom-call(s32[3,8]{1,0:T(4,128)} %bitcast.1, s32[1,3]{1,0:T(1,128)} %active.1, bf16[256,1024]{1,0:T(8,128)(2,1)} %q_in.1, bf16[256,1024]{1,0:T(8,128)(2,1)} %k_in.1, bf16[256,1024]{1,0:T(8,128)(2,1)} %v_in.1, ...), custom_call_target="tpu_custom_call" | custom-call | tf_op jit(solution)/shard_map/attention_grads/pallas_call | solution.py:459
  111.8 1.9 %copy.13 = bf16[256,1024]{1,0:T(8,128)(2,1)} copy(bf16[256,1024]{1,0:T(8,128)(2,1)} %get-tuple-element.6) | data formatting | bytes 1048576
  113.7 1.9 %copy.14 = bf16[256,1024]{1,0:T(8,128)(2,1)} copy(bf16[256,1024]{1,0:T(8,128)(2,1)} %get-tuple-element.7) | data formatting | bytes 1048576
  115.5 1.9 %copy.15 = bf16[256,1024]{1,0:T(8,128)(2,1)} copy(bf16[256,1024]{1,0:T(8,128)(2,1)} %get-tuple-element.8) | data formatting | bytes 1048576

commit v3 on v2

--- a/solution.py
+++ b/solution.py
@@ -41,6 +41,8 @@
         return {"seq": lax.rem(seq + (steps % 8) * stride, seq_count)}
 
     def cols(h):
+        if isinstance(h, int):
+            return pl.ds(h * HDIM, HDIM)
         return pl.ds(pl.multiple_of(h * HDIM, HDIM), HDIM)
 
     def remote(source, target, send, recv, device):
@@ -59,18 +61,28 @@
             along(sign * (2 if hop == 2 else 1)),
         )
 
-    def og_move(hop):
+    def half_of(half):
+        return pl.ds(half * (width // 2), width // 2)
+
+    def og_move(hop, half):
+        part = half_of(half)
         return remote(
-            og.at[hop, 0], og.at[hop + 1, 0], og_send.at[hop], og_recv.at[hop],
-            along(-(2 if hop == 2 else 1)),
-        )
-
-    def near(slot, which):
+            og.at[hop, 0, :, part], og.at[hop + 1, 0, :, part],
+            og_send.at[hop, half], og_recv.at[hop, half], along(-(2 if hop == 2 else 1)),
+        )
+
+    def near(slot, which, half):
         source, target, mate = ((0, 1, 1), (0, 2, 2), (2, 3, 1))[which]
+        part = half_of(half)
         return remote(
-            og.at[slot, source], og.at[slot, target], near_send.at[slot, which],
-            near_recv.at[slot, which], {"head": mates[mate]},
-        )
+            og.at[slot, source, :, part], og.at[slot, target, :, part],
+            near_send.at[slot, which, half], near_recv.at[slot, which, half],
+            {"head": mates[mate]},
+        )
+
+    def spread(slot, half):
+        near(slot, 1, half).start()
+        near(slot, 0, half).start()
 
     def stat_move(hop, h):
         return remote(
@@ -102,8 +114,9 @@
         return jnp.where(key_index <= query_index, raw, HIDE)
 
     def make_grad(slot):
-        near(slot, 0).wait_recv()
-        near(slot, 2).wait_recv()
+        for half in range(2):
+            near(slot, 0, half).wait_recv()
+            near(slot, 2, half).wait_recv()
 
         @pl.loop(0, heads // 2)
         def _(pair):
@@ -115,8 +128,15 @@
             ga[slot, :, wide] = total.astype(jnp.bfloat16)
 
     def pass_near(slot):
-        near(slot, 1).wait_recv()
-        near(slot, 2).start()
+        for half in range(2):
+            near(slot, 1, half).wait_recv()
+            near(slot, 2, half).start()
+
+    def pass_og(hop, half):
+        og_move(hop, half).wait_recv()
+        if hop < 2:
+            og_move(hop + 1, half).start()
+        spread(hop + 1, half)
 
     def query_side(h):
         at = cols(h)
@@ -290,158 +310,148 @@
     def each(first, last):
         return pl.loop(first, last)
 
+    def begin(kinds, hop, first, last):
+        @each(first, last)
+        def _(h):
+            for kind in kinds:
+                move(kind, hop, h).start()
+
+    def relay(kind, hop, h):
+        move(kind, hop, h).wait_recv()
+        move(kind, hop + 1, h).start()
+
+    def late_query_side(h):
+        move("k", 2, h).wait_recv()
+        move("v", 2, h).wait_recv()
+        query_side(h)
+
+    def late_key_side(h):
+        move("q", 2, h).wait_recv()
+        for hop in range(SECTIONS):
+            row_move(hop, h).wait_recv()
+        key_side(h)
+
+    def relay_kv(hop, h):
+        relay("k", hop, h)
+        relay("v", hop, h)
+
     copies[0].wait()
-    og_move(0).start()
-    near(0, 1).start()
-    near(0, 0).start()
-    copies[1].wait()
-
-    @each(0, 2)
-    def _(h):
-        move("q", 0, h).start()
-
+    for half in range(2):
+        og_move(0, half).start()
+    for half in range(2):
+        spread(0, half)
     copies[2].wait()
     copies[3].wait()
+    begin("kv", 0, moved, heads)
+    copies[1].wait()
+    pass_og(0, 0)
+    pass_og(0, 1)
+    begin("q", 0, 0, moved)
+    relay_kv(0, 4)
+    relay_kv(0, 5)
+    pass_og(1, 0)
+    relay_kv(0, 6)
+    pass_og(1, 1)
+    relay_kv(0, 7)
+    pass_near(0)
+    copies[4].wait()
+    make_grad(0)
+    for h in range(moved):
+        relay("q", 0, h)
+    pass_near(1)
+    make_grad(1)
+    relay_kv(1, 4)
+    relay_kv(1, 5)
+    pass_near(2)
+    make_grad(2)
+    relay_kv(1, 6)
+    pass_og(2, 0)
+    for h in range(moved):
+        stage_own(h)
+    pass_og(2, 1)
+    late_query_side(4)
+    for h in range(moved):
+        relay("q", 1, h)
+    late_query_side(5)
+    pass_near(3)
+    make_grad(3)
+    stage_a(0)
+    stage_a(1)
+    relay_kv(1, 7)
+    late_query_side(6)
+    stage_b(0)
+    begin("q", 0, 4, 6)
+    stage_a(2)
+    stage_b(1)
+    begin("q", 0, 6, 8)
+    stage_a(3)
+    late_query_side(7)
+    stage_b(2)
+    relay("q", 0, 4)
+    stage_c(0)
+    relay("q", 0, 5)
+    stage_c(1)
+    stage_b(3)
+    relay("q", 0, 6)
+    relay("q", 0, 7)
+    stage_c(2)
+    stage_back(0, 0)
+    relay("q", 1, 4)
+    stage_c(3)
+    relay("q", 1, 5)
+    stage_back(0, 1)
+    relay("q", 1, 6)
+    stage_back(1, 0)
+    stage_back(0, 2)
+    relay("q", 1, 7)
+    stage_back(1, 1)
+    late_key_side(4)
+    stage_back(0, 3)
+    stage_back(2, 0)
+    stage_back(1, 2)
+    late_key_side(5)
+    stage_back(2, 1)
+    stage_back(1, 3)
+    late_key_side(6)
+    stage_back(2, 2)
+    late_key_side(7)
+    stage_back(2, 3)
+
+    @each(0, heads)
+    def _(h):
+        for hop in range(SECTIONS):
+            row_move(hop, h).wait_send()
+            move("q", hop, h).wait_send()
+
+    @each(0, moved)
+    def _(h):
+        for hop in range(SECTIONS):
+            stat_move(hop, h).wait_send()
+            back_move(hop, h).wait_send()
 
     @each(moved, heads)
     def _(h):
-        move("k", 0, h).start()
-        move("v", 0, h).start()
-
-    og_move(0).wait_recv()
-    og_move(1).start()
-    near(1, 1).start()
-    near(1, 0).start()
-
-    @each(2, 4)
-    def _(h):
-        move("q", 0, h).start()
-
-    pass_near(0)
-
-    @each(0, 2)
-    def _(h):
-        move("q", 0, h).wait_recv()
-        move("q", 1, h).start()
-
-    @each(moved, heads)
-    def _(h):
-        for kind in "kv":
-            move(kind, 0, h).wait_recv()
-            move(kind, 1, h).start()
-
-    og_move(1).wait_recv()
-    og_move(2).start()
-    near(2, 1).start()
-    near(2, 0).start()
-
-    @each(4, heads)
-    def _(h):
-        move("q", 0, h).start()
-
-    pass_near(1)
-
-    @each(2, heads)
-    def _(h):
-        move("q", 0, h).wait_recv()
-        move("q", 1, h).start()
-
-    copies[4].wait()
-    make_grad(0)
-
-    @each(moved, heads)
-    def _(h):
-        for kind in "kv":
-            move(kind, 1, h).wait_recv()
-            move(kind, 2, h).start()
-
-    @each(0, 4)
-    def _(h):
-        move("q", 1, h).wait_recv()
-        move("q", 2, h).start()
-
-    pass_near(2)
-    og_move(2).wait_recv()
-    near(3, 1).start()
-    near(3, 0).start()
-
-    make_grad(1)
-    make_grad(2)
-
-    @each(4, heads)
-    def _(h):
-        move("q", 1, h).wait_recv()
-
-    @each(0, moved)
-    def _(h):
-        stage_own(h)
-
-    pass_near(3)
-
-    @each(moved, heads - 2)
-    def _(h):
-        for kind in "kv":
-            move(kind, 2, h).wait_recv()
-        query_side(h)
-
-    make_grad(3)
-
-    @each(heads - 2, heads)
-    def _(h):
-        for kind in "kv":
-            move(kind, 2, h).wait_recv()
-        query_side(h)
-
-    lag_b, lag_c, lag_d, lag_e, lag_f = 2, 3, 5, 7, 9
-    lead = 3
-
-    @each(0, moved + lag_f)
-    def _(step):
-        def when(low, high, action):
-            @pl.when((step >= low) & (step < high))
-            def _():
-                action(step - low)
-
-        when(1, 1 + heads - 4, lambda i: move("q", 2, i + 4).start())
-        when(0, moved, stage_a)
-        when(lag_b, lag_b + moved, stage_b)
-        when(lag_c, lag_c + moved, stage_c)
-        when(lag_d, lag_d + moved, lambda i: stage_back(0, i))
-        when(lag_e, lag_e + moved, lambda i: stage_back(1, i))
-        when(lag_f, lag_f + moved, lambda i: stage_back(2, i))
-
-        def last_heads(i):
-            h = i + moved
-            move("q", 2, h).wait_recv()
-            for hop in range(SECTIONS):
-                row_move(hop, h).wait_recv()
-            key_side(h)
-
-        when(moved + lead, heads + lead, last_heads)
-
-    @each(0, heads)
-    def _(h):
-        for hop in range(SECTIONS):
-            row_move(hop, h).wait_send()
-            move("q", hop, h).wait_send()
-
-    @each(0, moved)
-    def _(h):
-        for hop in range(SECTIONS):
-            stat_move(hop, h).wait_send()
-            back_move(hop, h).wait_send()
-
-    @each(moved, heads)
-    def _(h):
         for hop in range(SECTIONS):
             for kind in "kv":
                 move(kind, hop, h).wait_send()
 
-    for hop in range(SECTIONS):
-        og_move(hop).wait_send()
-    for slot in range(SECTIONS + 1):
-        for which in range(3):
-            near(slot, which).wait_send()
+    for half in range(2):
+        for hop in range(SECTIONS):
+            og_move(hop, half).wait_send()
+        for slot in range(SECTIONS + 1):
+            for which in range(3):
+                near(slot, which, half).wait_send()
+
+
+def write_out(dq, dk, dv, dq_out, dk_out, dv_out, sem):
+    copies = [
+        pltpu.make_async_copy(source, target, sem.at[index])
+        for index, (source, target) in enumerate(((dq, dq_out), (dk, dk_out), (dv, dv_out)))
+    ]
+    for copy in copies:
+        copy.start()
+    for copy in copies:
+        copy.wait()
 
 
 def body(queries, key_rows, value_rows, out_grad, out_proj, section_table, block_active):
@@ -456,10 +466,16 @@
     smem = pl.BlockSpec(memory_space=pltpu.SMEM)
     out = jax.ShapeDtypeStruct((BLK, width), jnp.bfloat16)
     bf16, f32, dma = jnp.bfloat16, jnp.float32, pltpu.SemaphoreType.DMA
-    return pl.pallas_call(
+    placed = [
+        pltpu.with_memory_space_constraint(array, pltpu.HBM)
+        for array in (
+            section_table.T, block_active, queries, key_rows, value_rows, out_grad, out_proj
+        )
+    ]
+    grads = pl.pallas_call(
         functools.partial(kernel, seq_count, moved),
         out_shape=(out, out, out),
-        in_specs=[smem, smem] + [any_space] * 5,
+        in_specs=[smem, smem] + [pl.BlockSpec(memory_space=pltpu.HBM)] * 5,
         out_specs=(vmem, vmem, vmem),
         scratch_shapes=[
             pltpu.VMEM(four, bf16),
@@ -484,10 +500,10 @@
             pltpu.VMEM((SECTIONS, BLK, part), bf16),
             pltpu.VMEM((SECTIONS, BLK, part), bf16),
             dma((5,)),
-            dma((SECTIONS,)),
-            dma((SECTIONS,)),
-            dma((SECTIONS + 1, 3)),
-            dma((SECTIONS + 1, 3)),
+            dma((SECTIONS, 2)),
+            dma((SECTIONS, 2)),
+            dma((SECTIONS + 1, 3, 2)),
+            dma((SECTIONS + 1, 3, 2)),
             dma((3, SECTIONS, heads)),
             dma((3, SECTIONS, heads)),
             dma((SECTIONS, moved)),
@@ -498,10 +514,19 @@
             dma((SECTIONS, moved)),
         ],
         compiler_params=pltpu.CompilerParams(
-            collective_id=0, has_side_effects=True, vmem_limit_bytes=60 * 1024 * 1024
+            collective_id=0, has_side_effects=True, vmem_limit_bytes=44 * 1024 * 1024
         ),
         name="attention_grads",
-    )(section_table.T, block_active, queries, key_rows, value_rows, out_grad, out_proj)
+    )(*placed)
+    return pl.pallas_call(
+        write_out,
+        out_shape=(out, out, out),
+        in_specs=[vmem] * 3,
+        out_specs=[any_space] * 3,
+        scratch_shapes=[dma((3,))],
+        compiler_params=pltpu.CompilerParams(vmem_limit_bytes=4 * 1024 * 1024),
+        name="write_out",
+    )(*grads)
 
 
 def solution(mesh):

time: 118 us -> 95 us (0.81); the launches traced: 117 us -> 93.2 us
  Pallas kernels: 111 us -> 92.4 us
  local copies, waits for them, and re-layouts: 5.6 us -> 0 us
    pallas_call x1, Pallas kernels: 111 us -> 91.2 us  [body(): pl.pallas_call(functools.partial(kernel, seq_count, moved), out_shape=(ou...]
    unnamed x3 -> x0, local copies, waits for them, and re-layouts: 5.6 us -> none
where the time goes in v3:
time: 95 us; the launch traced here: 93.2 us
  Pallas kernels  92.4 us (97%)
    pallas_call x1, Pallas kernels, body(): pl.pallas_call(functools.partial(kernel, seq_count, moved), out_shape=(ou...  91.2 us

profile of v3, /device:TPU:60, one launch (start us, length us, event | category | flops | bytes accessed | tf_op | source)
XLA Modules:
  0.0 93.2 jit_solution(5990358928353673650)
XLA Ops:
  0.6 91.2 %attention_grads.1 = (bf16[256,1024]{1,0:T(8,128)(2,1)S(1)}, bf16[256,1024]{1,0:T(8,128)(2,1)S(1)}, bf16[256,1024]{1,0:T(8,128)(2,1)S(1)}) custom-call(s32[3,8]{1,0:T(4,128)} %bitcast.1, s32[1,3]{1,0:T(1,128)} %active.1, bf16[256,1024]{1,0:T(8,128)(2,1)} %q_in.1, bf16[256,1024]{1,0:T(8,128)(2,1)} %k_in.1, bf16[256,1024]{1,0:T(8,128)(2,1)} %v_in.1, ...), custom_call_target="tpu_custom_call" | custom-call | tf_op jit(solution)/shard_map/attention_grads/pallas_call | solution.py:475
  91.9 1.2 %write_out.1 = (bf16[256,1024]{1,0:T(8,128)(2,1)}, bf16[256,1024]{1,0:T(8,128)(2,1)}, bf16[256,1024]{1,0:T(8,128)(2,1)}) custom-call(bf16[256,1024]{1,0:T(8,128)(2,1)S(1)} %get-tuple-element.6.dq, bf16[256,1024]{1,0:T(8,128)(2,1)S(1)} %get-tuple-element.7.dk, bf16[256,1024]{1,0:T(8,128)(2,1)S(1)} %get-tuple-element.8.dv), custom_call_target="tpu_custom_call" | custom-call | tf_op jit(solution)/shard_map/write_out/pallas_call | solution.py:521

commit v4 on v3

--- a/solution.py
+++ b/solution.py
@@ -11,6 +11,10 @@
 BLK = 256
 HDIM = 128
 SECTIONS = 3
+PARTS = 4
+MODE = "open"
+KV_WRAP = True
+OG_WRAP = True
 MESH = pl.DeviceIdType.MESH
 HIDE = -1e30
 SCALE = 1.0 / math.sqrt(HDIM)
@@ -19,15 +23,25 @@
 NN = (((1,), (0,)), ((), ()))
 
 
+def given(condition):
+    if isinstance(condition, bool):
+        return (lambda action: action()) if condition else (lambda action: None)
+    return pl.when(condition)
+
+
+def opposite(condition):
+    return not condition if isinstance(condition, bool) else jnp.logical_not(condition)
+
+
 def mm(a, b, dims):
     return lax.dot_general(a, b, dims, preferred_element_type=jnp.float32)
 
 
 def kernel(
     seq_count, moved, table, active, q_in, k_in, v_in, og_in, w_in, dq, dk, dv,
-    qa, ga, ka, va, og, w, scores, slopes, held_p, held_s, tops, norms, own_dk, own_dv, parts,
+    qa, ga, ka, va, og, og_wrap, kv_wrap, w, scores, slopes, held_p, held_s, tops, norms, own_dk, own_dv, parts,
     stat_out, stat_in, row_out, row_in, back_out, back_in,
-    local_sem, og_send, og_recv, near_send, near_recv, bulk_send, bulk_recv,
+    local_sem, og_send, og_recv, hop_send, hop_recv, wrap_send, wrap_recv, near_send, near_recv, bulk_send, bulk_recv,
     stat_send, stat_recv, row_send, row_recv, back_send, back_recv,
 ):
     heads = q_in.shape[1] // HDIM
@@ -35,6 +49,24 @@
     seq = lax.axis_index("seq")
     me = lax.axis_index("head")
     stride = seq_count // 8
+    z = seq // stride
+    far = (1, 2, 4)
+    if MODE == "cyclic":
+        above = below = [True] * 3
+        down_send = up_send = og_sends = back_send_if = back_recv_if = (True, True, True)
+    else:
+        above = [z + steps <= 7 for steps in far]
+        below = [z >= steps for steps in far]
+        middle = (z >= 2) & (z <= 5)
+        down_send = (z >= 1, (z >= 1) & (z <= 6), middle)
+        up_send = (z <= 6, (z >= 1) & (z <= 6), (z == 2) | (z == 4) | (z == 5) if KV_WRAP else middle)
+        og_sends = (z >= 1, (z >= 1) & (z <= 6), (z == 2) | (z == 5) if OG_WRAP else middle)
+        back_send_if = (z <= 3, z <= 5, z <= 6)
+        back_recv_if = (middle, (z >= 1) & (z <= 6), z >= 1)
+    og_forward = (z == 7) | (z == 0) if OG_WRAP else False
+    og_leaves = (z == 5) | (z == 6) if OG_WRAP else False
+    kv_leaves = z == 1 if KV_WRAP else False
+    kv_forward = z == 7 if KV_WRAP else False
     mates = (me, me + 1 - 2 * (me % 2), me + 2 - 4 * (me // 2), 3 - me)
 
     def along(steps):
@@ -62,7 +94,7 @@
         )
 
     def half_of(half):
-        return pl.ds(half * (width // 2), width // 2)
+        return pl.ds(half * (width // PARTS), width // PARTS)
 
     def og_move(hop, half):
         part = half_of(half)
@@ -70,6 +102,55 @@
             og.at[hop, 0, :, part], og.at[hop + 1, 0, :, part],
             og_send.at[hop, half], og_recv.at[hop, half], along(-(2 if hop == 2 else 1)),
         )
+
+    def og_out(half):
+        part = half_of(half)
+        return remote(
+            og.at[0, 0, :, part], og_wrap.at[:, part],
+            hop_send.at[half], hop_recv.at[half], along(2),
+        )
+
+    def og_on(half):
+        part = half_of(half)
+        return remote(
+            og_wrap.at[:, part], og.at[3, 0, :, part],
+            og_send.at[2, half], og_recv.at[2, half], along(2),
+        )
+
+    def kv_out(index, h):
+        ref = (ka, va)[index]
+        return remote(
+            ref.at[0, :, cols(h)], kv_wrap.at[index, :, cols(h - moved)],
+            wrap_send.at[index, h], wrap_recv.at[index, h], along(-2),
+        )
+
+    def kv_on(index, h):
+        ref = (ka, va)[index]
+        return remote(
+            kv_wrap.at[index, :, cols(h - moved)], ref.at[3, :, cols(h)],
+            bulk_send.at[index, 2, h], bulk_recv.at[index, 2, h], along(-2),
+        )
+
+    def sends(kind, hop):
+        return (down_send if kind == "q" else up_send)[hop]
+
+    def comes(kind, hop):
+        return (above if kind == "q" else below)[hop]
+
+    def started(condition, copy):
+        @given(condition)
+        def _():
+            copy().start()
+
+    def landed(condition, copy):
+        @given(condition)
+        def _():
+            copy().wait_recv()
+
+    def left(condition, copy):
+        @given(condition)
+        def _():
+            copy().wait_send()
 
     def near(slot, which, half):
         source, target, mate = ((0, 1, 1), (0, 2, 2), (2, 3, 1))[which]
@@ -113,30 +194,54 @@
         query_index = lax.broadcasted_iota(jnp.int32, (BLK, BLK), 1)
         return jnp.where(key_index <= query_index, raw, HIDE)
 
+    def slot_used(slot):
+        return True if slot == 0 else above[slot - 1]
+
     def make_grad(slot):
-        for half in range(2):
-            near(slot, 0, half).wait_recv()
-            near(slot, 2, half).wait_recv()
-
-        @pl.loop(0, heads // 2)
-        def _(pair):
-            wide = pl.ds(pl.multiple_of(pair * 2 * HDIM, 2 * HDIM), 2 * HDIM)
-            total = jnp.zeros((BLK, 2 * HDIM), jnp.float32)
-            for index, owner in enumerate(mates):
-                features = pl.ds(pl.multiple_of(owner * width, width), width)
-                total = total + mm(og[slot, index], w[wide, features], NT)
-            ga[slot, :, wide] = total.astype(jnp.bfloat16)
+        @given(slot_used(slot))
+        def _():
+            for half in range(PARTS):
+                near(slot, 0, half).wait_recv()
+                near(slot, 2, half).wait_recv()
+
+            @pl.loop(0, heads // 2)
+            def _(pair):
+                wide = pl.ds(pl.multiple_of(pair * 2 * HDIM, 2 * HDIM), 2 * HDIM)
+                total = jnp.zeros((BLK, 2 * HDIM), jnp.float32)
+                for index, owner in enumerate(mates):
+                    features = pl.ds(pl.multiple_of(owner * width, width), width)
+                    total = total + mm(og[slot, index], w[wide, features], NT)
+                ga[slot, :, wide] = total.astype(jnp.bfloat16)
 
     def pass_near(slot):
-        for half in range(2):
-            near(slot, 1, half).wait_recv()
-            near(slot, 2, half).start()
+        @given(slot_used(slot))
+        def _():
+            for half in range(PARTS):
+                near(slot, 1, half).wait_recv()
+                near(slot, 2, half).start()
 
     def pass_og(hop, half):
-        og_move(hop, half).wait_recv()
+        @given(above[hop])
+        def _():
+            og_move(hop, half).wait_recv()
         if hop < 2:
-            og_move(hop + 1, half).start()
-        spread(hop + 1, half)
+            started(og_sends[hop + 1], lambda: og_move(hop + 1, half))
+        @given(above[hop])
+        def _():
+            spread(hop + 1, half)
+
+    def forward_og(half):
+        @given(og_forward)
+        def _():
+            og_out(half).wait_recv()
+            og_on(half).start()
+
+    def forward_kv(h):
+        @given(kv_forward)
+        def _():
+            for index in range(2):
+                kv_out(index, h).wait_recv()
+                kv_on(index, h).start()
 
     def query_side(h):
         at = cols(h)
@@ -180,7 +285,7 @@
                 own_dk[:, at] = mm(dlogit, query, NN)
         dq[:, at] = query_sum.astype(jnp.bfloat16)
         for hop in range(SECTIONS):
-            row_move(hop, h).start()
+            started(below[hop], lambda hop=hop: row_move(hop, h))
 
     def key_side(h):
         at = cols(h)
@@ -222,19 +327,18 @@
         norms[h, 1:2, :] = drift
 
     def stage_a(h):
-        for kind in ("q",):
-            move(kind, 2, h).wait_recv()
+        landed(comes("q", 2), lambda: move("q", 2, h))
         for hop in range(SECTIONS):
             top, total, drift = partial_scores(hop + 1, h)
             stat_out[hop, h, 0:1, :] = top
             stat_out[hop, h, 1:2, :] = total
             stat_out[hop, h, 2:3, :] = drift
             stat_out[hop, h, 3:4, :] = drift
-            stat_move(hop, h).start()
+            started(above[hop], lambda hop=hop: stat_move(hop, h))
 
     def stage_b(h):
         for hop in range(SECTIONS):
-            stat_move(hop, h).wait_recv()
+            landed(below[hop], lambda hop=hop: stat_move(hop, h))
         tops_of = [tops[0, h, 0:1, :]] + [
             stat_in[hop, h, 0:1, :] + hidden(hop, h) for hop in range(SECTIONS)
         ]
@@ -253,12 +357,12 @@
         for hop in range(SECTIONS):
             row_out[hop, h, 0:1, :] = log_norm - hidden(hop, h)
             row_out[hop, h, 1:2, :] = delta
-            row_move(hop, h).start()
+            started(below[hop], lambda hop=hop: row_move(hop, h))
 
     def stage_c(h):
         at = cols(h)
         for hop in range(SECTIONS):
-            row_move(hop, h).wait_recv()
+            landed(above[hop], lambda hop=hop: row_move(hop, h))
         key_sum = None
         value_sum = None
         for slot in (3, 2, 1, 0):
@@ -279,17 +383,17 @@
             value_sum = value_part if value_sum is None else value_sum + value_part
         dk[:, at] = key_sum.astype(jnp.bfloat16)
         dv[:, at] = value_sum.astype(jnp.bfloat16)
-        back_move(0, h).start()
+        started(back_send_if[0], lambda: back_move(0, h))
 
     def stage_back(hop, h):
         at = cols(h)
-        back_move(hop, h).wait_recv()
+        landed(back_recv_if[hop], lambda: back_move(hop, h))
         total = (parts[2 - hop, :, at] + back_in[hop, :, at].astype(jnp.float32)).astype(jnp.bfloat16)
         if hop == 2:
             dq[:, at] = total
         else:
             back_out[hop + 1, :, at] = total
-            back_move(hop + 1, h).start()
+            started(back_send_if[hop + 1], lambda: back_move(hop + 1, h))
 
     copies = [
         pltpu.make_async_copy(source, target, local_sem.at[index])
@@ -299,6 +403,26 @@
     ]
     for copy in copies:
         copy.start()
+
+    def fill(ref, value=0.0):
+        ref[...] = jnp.full(ref.shape, value, ref.dtype)
+
+    for slot in range(1, SECTIONS + 1):
+        @given(opposite(above[slot - 1]))
+        def _(slot=slot):
+            fill(qa.at[slot])
+            fill(ga.at[slot])
+            fill(row_in.at[slot - 1], -HIDE)
+
+        @given(opposite(below[slot - 1]))
+        def _(slot=slot):
+            fill(ka.at[slot])
+            fill(va.at[slot])
+            fill(stat_in.at[slot - 1])
+
+        @given(opposite(back_recv_if[slot - 1]))
+        def _(slot=slot):
+            fill(back_in.at[slot - 1])
 
     barrier = pltpu.get_barrier_semaphore()
     for steps in (1, -1, 2, -2, 4):
@@ -311,136 +435,174 @@
         return pl.loop(first, last)
 
     def begin(kinds, hop, first, last):
-        @each(first, last)
-        def _(h):
-            for kind in kinds:
-                move(kind, hop, h).start()
+        @given(sends(kinds[0], hop))
+        def _():
+            @each(first, last)
+            def _(h):
+                for kind in kinds:
+                    move(kind, hop, h).start()
 
     def relay(kind, hop, h):
-        move(kind, hop, h).wait_recv()
-        move(kind, hop + 1, h).start()
+        landed(comes(kind, hop), lambda: move(kind, hop, h))
+        started(sends(kind, hop + 1), lambda: move(kind, hop + 1, h))
 
     def late_query_side(h):
-        move("k", 2, h).wait_recv()
-        move("v", 2, h).wait_recv()
+        for kind in "kv":
+            landed(comes(kind, 2), lambda kind=kind: move(kind, 2, h))
         query_side(h)
 
     def late_key_side(h):
-        move("q", 2, h).wait_recv()
-        for hop in range(SECTIONS):
-            row_move(hop, h).wait_recv()
+        landed(comes("q", 2), lambda: move("q", 2, h))
+        for hop in range(SECTIONS):
+            landed(above[hop], lambda hop=hop: row_move(hop, h))
         key_side(h)
 
     def relay_kv(hop, h):
         relay("k", hop, h)
         relay("v", hop, h)
 
+    def send_kv_round(first, last):
+        @given(kv_leaves)
+        def _():
+            @each(first, last)
+            def _(h):
+                kv_out(0, h).start()
+                kv_out(1, h).start()
+
     copies[0].wait()
-    for half in range(2):
-        og_move(0, half).start()
-    for half in range(2):
+    for half in range(PARTS):
+        started(og_sends[0], lambda half=half: og_move(0, half))
+    for half in range(PARTS):
         spread(0, half)
+    for half in range(PARTS):
+        started(og_leaves, lambda half=half: og_out(half))
     copies[2].wait()
     copies[3].wait()
     begin("kv", 0, moved, heads)
     copies[1].wait()
     pass_og(0, 0)
     pass_og(0, 1)
-    begin("q", 0, 0, moved)
+    pass_og(0, 2)
+    pass_og(0, 3)
+    begin("q", 0, 0, 4)
+    pass_og(1, 0)
+    forward_og(0)
+    pass_og(1, 1)
+    forward_og(1)
     relay_kv(0, 4)
+    pass_og(1, 2)
+    forward_og(2)
+    pass_og(1, 3)
+    forward_og(3)
     relay_kv(0, 5)
-    pass_og(1, 0)
     relay_kv(0, 6)
-    pass_og(1, 1)
     relay_kv(0, 7)
     pass_near(0)
     copies[4].wait()
     make_grad(0)
-    for h in range(moved):
-        relay("q", 0, h)
     pass_near(1)
+    relay("q", 0, 0)
+    relay("q", 0, 1)
+    relay("q", 0, 2)
+    relay("q", 0, 3)
+    send_kv_round(4, 6)
     make_grad(1)
-    relay_kv(1, 4)
-    relay_kv(1, 5)
+    pass_og(2, 0)
+    pass_og(2, 1)
+    stage_own(0)
+    stage_own(1)
+    stage_own(2)
+    stage_own(3)
+    pass_og(2, 2)
+    pass_og(2, 3)
     pass_near(2)
     make_grad(2)
-    relay_kv(1, 6)
-    pass_og(2, 0)
-    for h in range(moved):
-        stage_own(h)
-    pass_og(2, 1)
-    late_query_side(4)
-    for h in range(moved):
-        relay("q", 1, h)
-    late_query_side(5)
+    relay("q", 1, 0)
+    relay("q", 1, 1)
+    relay("q", 1, 2)
     pass_near(3)
     make_grad(3)
     stage_a(0)
+    relay_kv(1, 4)
     stage_a(1)
+    relay("q", 1, 3)
+    send_kv_round(6, 8)
+    relay_kv(1, 5)
+    forward_kv(4)
+    stage_b(0)
+    begin("q", 0, 4, 8)
+    forward_kv(5)
+    stage_a(2)
+    relay_kv(1, 6)
+    stage_b(1)
+    stage_a(3)
     relay_kv(1, 7)
-    late_query_side(6)
-    stage_b(0)
-    begin("q", 0, 4, 6)
-    stage_a(2)
-    stage_b(1)
-    begin("q", 0, 6, 8)
-    stage_a(3)
-    late_query_side(7)
+    forward_kv(6)
+    relay("q", 0, 4)
     stage_b(2)
-    relay("q", 0, 4)
+    relay("q", 0, 5)
     stage_c(0)
-    relay("q", 0, 5)
+    stage_b(3)
+    forward_kv(7)
+    relay("q", 0, 6)
     stage_c(1)
-    stage_b(3)
-    relay("q", 0, 6)
     relay("q", 0, 7)
+    late_query_side(4)
+    relay("q", 1, 4)
+    stage_back(0, 0)
     stage_c(2)
-    stage_back(0, 0)
-    relay("q", 1, 4)
+    relay("q", 1, 5)
+    late_query_side(5)
     stage_c(3)
-    relay("q", 1, 5)
     stage_back(0, 1)
     relay("q", 1, 6)
     stage_back(1, 0)
+    late_query_side(6)
+    relay("q", 1, 7)
     stage_back(0, 2)
-    relay("q", 1, 7)
     stage_back(1, 1)
-    late_key_side(4)
+    late_query_side(7)
     stage_back(0, 3)
     stage_back(2, 0)
     stage_back(1, 2)
-    late_key_side(5)
+    late_key_side(4)
     stage_back(2, 1)
     stage_back(1, 3)
+    late_key_side(5)
+    stage_back(2, 2)
     late_key_side(6)
-    stage_back(2, 2)
+    stage_back(2, 3)
     late_key_side(7)
-    stage_back(2, 3)
 
     @each(0, heads)
     def _(h):
         for hop in range(SECTIONS):
-            row_move(hop, h).wait_send()
-            move("q", hop, h).wait_send()
+            left(below[hop], lambda hop=hop: row_move(hop, h))
+            left(down_send[hop], lambda hop=hop: move("q", hop, h))
 
     @each(0, moved)
     def _(h):
         for hop in range(SECTIONS):
-            stat_move(hop, h).wait_send()
-            back_move(hop, h).wait_send()
+            left(above[hop], lambda hop=hop: stat_move(hop, h))
+            left(back_send_if[hop], lambda hop=hop: back_move(hop, h))
 
     @each(moved, heads)
     def _(h):
         for hop in range(SECTIONS):
             for kind in "kv":
-                move(kind, hop, h).wait_send()
-
-    for half in range(2):
-        for hop in range(SECTIONS):
-            og_move(hop, half).wait_send()
+                left(up_send[hop], lambda kind=kind, hop=hop: move(kind, hop, h))
+        for index in range(2):
+            left(kv_leaves, lambda index=index: kv_out(index, h))
+            left(kv_forward, lambda index=index: kv_on(index, h))
+
+    for half in range(PARTS):
+        left(og_leaves, lambda half=half: og_out(half))
+        left(og_forward, lambda half=half: og_on(half))
+        for hop in range(SECTIONS):
+            left(og_sends[hop], lambda hop=hop, half=half: og_move(hop, half))
         for slot in range(SECTIONS + 1):
             for which in range(3):
-                near(slot, which, half).wait_send()
+                left(slot_used(slot), lambda slot=slot, which=which, half=half: near(slot, which, half))
 
 
 def write_out(dq, dk, dv, dq_out, dk_out, dv_out, sem):
@@ -483,6 +645,8 @@
             pltpu.VMEM(four, bf16),
             pltpu.VMEM(four, bf16),
             pltpu.VMEM((SECTIONS + 1, 4, *out_grad.shape), bf16),
+            pltpu.VMEM(out_grad.shape, bf16),
+            pltpu.VMEM((2, BLK, width - part), bf16),
             pltpu.VMEM(out_proj.shape, bf16),
             pltpu.VMEM((SECTIONS + 1, BLK, BLK), f32),
             pltpu.VMEM((SECTIONS + 1, BLK, BLK), f32),
@@ -500,10 +664,14 @@
             pltpu.VMEM((SECTIONS, BLK, part), bf16),
             pltpu.VMEM((SECTIONS, BLK, part), bf16),
             dma((5,)),
-            dma((SECTIONS, 2)),
-            dma((SECTIONS, 2)),
-            dma((SECTIONS + 1, 3, 2)),
-            dma((SECTIONS + 1, 3, 2)),
+            dma((SECTIONS, PARTS)),
+            dma((SECTIONS, PARTS)),
+            dma((PARTS,)),
+            dma((PARTS,)),
+            dma((2, heads)),
+            dma((2, heads)),
+            dma((SECTIONS + 1, 3, PARTS)),
+            dma((SECTIONS + 1, 3, PARTS)),
             dma((3, SECTIONS, heads)),
             dma((3, SECTIONS, heads)),
             dma((SECTIONS, moved)),

time: 95 us -> 89.4 us (0.941)
  Pallas kernels: 92.4 us -> 87 us
    pallas_call x1, Pallas kernels: 91.2 us -> 85.9 us  [body(): pl.pallas_call(functools.partial(kernel, seq_count, moved), out_shape=(ou...]
where the time goes in v4:
time: 89.4 us; the launch traced here: 87.8 us
  Pallas kernels  87 us (97%)
    pallas_call x1, Pallas kernels, body(): pl.pallas_call(functools.partial(kernel, seq_count, moved), out_shape=(ou...  85.9 us

profile of v4, /device:TPU:60, one launch (start us, length us, event | category | flops | bytes accessed | tf_op | source)
XLA Modules:
  0.0 87.8 jit_solution(11522453986495269486)
XLA Ops:
  0.6 85.9 %attention_grads.1 = (bf16[256,1024]{1,0:T(8,128)(2,1)S(1)}, bf16[256,1024]{1,0:T(8,128)(2,1)S(1)}, bf16[256,1024]{1,0:T(8,128)(2,1)S(1)}) custom-call(s32[3,8]{1,0:T(4,128)} %bitcast.1, s32[1,3]{1,0:T(1,128)} %active.1, bf16[256,1024]{1,0:T(8,128)(2,1)} %q_in.1, bf16[256,1024]{1,0:T(8,128)(2,1)} %k_in.1, bf16[256,1024]{1,0:T(8,128)(2,1)} %v_in.1, ...), custom_call_target="tpu_custom_call" | custom-call | tf_op jit(solution)/shard_map/attention_grads/pallas_call | solution.py:637
  86.5 1.2 %write_out.1 = (bf16[256,1024]{1,0:T(8,128)(2,1)}, bf16[256,1024]{1,0:T(8,128)(2,1)}, bf16[256,1024]{1,0:T(8,128)(2,1)}) custom-call(bf16[256,1024]{1,0:T(8,128)(2,1)S(1)} %get-tuple-element.6.dq, bf16[256,1024]{1,0:T(8,128)(2,1)S(1)} %get-tuple-element.7.dk, bf16[256,1024]{1,0:T(8,128)(2,1)S(1)} %get-tuple-element.8.dv), custom_call_target="tpu_custom_call" | custom-call | tf_op jit(solution)/shard_map/write_out/pallas_call | solution.py:689

commit v5 on v4

--- a/solution.py
+++ b/solution.py
@@ -12,6 +12,7 @@
 HDIM = 128
 SECTIONS = 3
 PARTS = 4
+EARLY = 6
 MODE = "open"
 KV_WRAP = True
 OG_WRAP = True
@@ -434,8 +435,8 @@
     def each(first, last):
         return pl.loop(first, last)
 
-    def begin(kinds, hop, first, last):
-        @given(sends(kinds[0], hop))
+    def begin(kinds, hop, first, last, condition=None):
+        @given(sends(kinds[0], hop) if condition is None else condition)
         def _():
             @each(first, last)
             def _(h):
@@ -485,6 +486,7 @@
     pass_og(0, 2)
     pass_og(0, 3)
     begin("q", 0, 0, 4)
+    begin("q", 0, 4, 8, z >= EARLY)
     pass_og(1, 0)
     forward_og(0)
     pass_og(1, 1)
@@ -495,11 +497,11 @@
     pass_og(1, 3)
     forward_og(3)
     relay_kv(0, 5)
-    relay_kv(0, 6)
-    relay_kv(0, 7)
     pass_near(0)
     copies[4].wait()
     make_grad(0)
+    relay_kv(0, 6)
+    relay_kv(0, 7)
     pass_near(1)
     relay("q", 0, 0)
     relay("q", 0, 1)
@@ -515,9 +517,9 @@
     stage_own(3)
     pass_og(2, 2)
     pass_og(2, 3)
+    relay("q", 1, 0)
     pass_near(2)
     make_grad(2)
-    relay("q", 1, 0)
     relay("q", 1, 1)
     relay("q", 1, 2)
     pass_near(3)
@@ -526,42 +528,43 @@
     relay_kv(1, 4)
     stage_a(1)
     relay("q", 1, 3)
-    send_kv_round(6, 8)
+    begin("q", 0, 4, 6, (z >= 1) & (z < EARLY))
     relay_kv(1, 5)
     forward_kv(4)
     stage_b(0)
-    begin("q", 0, 4, 8)
+    begin("q", 0, 6, 8, (z >= 1) & (z < EARLY))
     forward_kv(5)
     stage_a(2)
     relay_kv(1, 6)
     stage_b(1)
+    relay("q", 0, 4)
     stage_a(3)
+    relay("q", 0, 5)
+    send_kv_round(6, 8)
     relay_kv(1, 7)
+    late_query_side(4)
+    stage_b(2)
+    relay("q", 0, 6)
+    stage_c(0)
+    late_query_side(5)
+    stage_b(3)
+    relay("q", 0, 7)
+    stage_c(1)
     forward_kv(6)
-    relay("q", 0, 4)
-    stage_b(2)
-    relay("q", 0, 5)
-    stage_c(0)
-    stage_b(3)
-    forward_kv(7)
-    relay("q", 0, 6)
-    stage_c(1)
-    relay("q", 0, 7)
-    late_query_side(4)
     relay("q", 1, 4)
     stage_back(0, 0)
+    relay("q", 1, 5)
     stage_c(2)
-    relay("q", 1, 5)
-    late_query_side(5)
+    forward_kv(7)
+    relay("q", 1, 6)
+    late_query_side(6)
     stage_c(3)
+    relay("q", 1, 7)
+    late_query_side(7)
     stage_back(0, 1)
-    relay("q", 1, 6)
     stage_back(1, 0)
-    late_query_side(6)
-    relay("q", 1, 7)
     stage_back(0, 2)
     stage_back(1, 1)
-    late_query_side(7)
     stage_back(0, 3)
     stage_back(2, 0)
     stage_back(1, 2)

time: 89.4 us -> 87.6 us (0.980); the launches traced: 87.8 us -> 87 us
  no operation moved by 1% of the time
where the time goes in v5:
time: 87.6 us; the launch traced here: 87 us
  Pallas kernels  86.2 us (98%)
    pallas_call x1, Pallas kernels, body(): pl.pallas_call(functools.partial(kernel, seq_count, moved), out_shape=(ou...  85 us

profile of v5, /device:TPU:60, one launch (start us, length us, event | category | flops | bytes accessed | tf_op | source)
XLA Modules:
  0.0 87.0 jit_solution(14536843742907089222)
XLA Ops:
  0.6 85.0 %attention_grads.1 = (bf16[256,1024]{1,0:T(8,128)(2,1)S(1)}, bf16[256,1024]{1,0:T(8,128)(2,1)S(1)}, bf16[256,1024]{1,0:T(8,128)(2,1)S(1)}) custom-call(s32[3,8]{1,0:T(4,128)} %bitcast.1, s32[1,3]{1,0:T(1,128)} %active.1, bf16[256,1024]{1,0:T(8,128)(2,1)} %q_in.1, bf16[256,1024]{1,0:T(8,128)(2,1)} %k_in.1, bf16[256,1024]{1,0:T(8,128)(2,1)} %v_in.1, ...), custom_call_target="tpu_custom_call" | custom-call | tf_op jit(solution)/shard_map/attention_grads/pallas_call | solution.py:640
  85.7 1.2 %write_out.1 = (bf16[256,1024]{1,0:T(8,128)(2,1)}, bf16[256,1024]{1,0:T(8,128)(2,1)}, bf16[256,1024]{1,0:T(8,128)(2,1)}) custom-call(bf16[256,1024]{1,0:T(8,128)(2,1)S(1)} %get-tuple-element.6.dq, bf16[256,1024]{1,0:T(8,128)(2,1)S(1)} %get-tuple-element.7.dk, bf16[256,1024]{1,0:T(8,128)(2,1)S(1)} %get-tuple-element.8.dv), custom_call_target="tpu_custom_call" | custom-call | tf_op jit(solution)/shard_map/write_out/pallas_call | solution.py:692
